TPU v7x, 128 devices: a whole 4x4x4 slice. The times are simulated.
128 devices in a mesh: dp: 16 (over y, x_lo, core), tensor: 8 (over z, x_hi).
Axes of the slice: x: 4 (x_hi: 2, x_lo: 2; x = x_hi * 2 + x_lo), y: 4, z: 4, core: 2. Of those that a mesh axis runs over, the one named last changes fastest.
Arguments:
- arrived: bfloat16 [256, 128, 1536], P(('dp', 'tensor')), may hold values from -6 to 6
- destination: int32 [256], replicated, may hold values from 0 to 15, as said below
- query_of: int32 [256], replicated, may hold values from 0 to 31, as said below
- lengths: int32 [256], replicated, may hold values from 32 to 128
- attn_gain: float32 [1536], replicated, may hold values from 0.25 to 1.75
- q_weight: bfloat16 [1536, 1024], P(None, 'tensor')
- q_bias: bfloat16 [1024], P('tensor'), may hold values from -3 to 3
- k_weight: bfloat16 [1536, 256], replicated
- v_weight: bfloat16 [1536, 256], replicated, may hold values from -0.15625 to 0.15625
- v_bias: bfloat16 [256], replicated, may hold values from -3 to 3
- o_weight: bfloat16 [1024, 1536], P('tensor'), may hold values from -0.1875 to 0.1875
- mlp_gain: float32 [1536], replicated, may hold values from 0.25 to 1.75
- w_gate: bfloat16 [1536, 8960], P(None, 'tensor'), may hold values from -0.15625 to 0.15625
- w_up: bfloat16 [1536, 8960], P(None, 'tensor'), may hold values from -0.15625 to 0.15625
- w_down: bfloat16 [8960, 1536], P('tensor'), may hold values from -0.0625 to 0.0625
- final_gain: float32 [1536], replicated, may hold values from 0.25 to 1.75
- score_weight: float32 [1536], replicated, may hold values from -0.15625 to 0.15625
Outputs:
- hidden_out: bfloat16 [128, 256, 1536], P('tensor', 'dp')
- centred: float32 [256], P('dp')
- query_mean: float32 [32], P('dp')
Inputs may be any that keep to these rules, and one draw needn't show every extreme that they name: In each aligned block of 16 pairs every destination occurs exactly once. `query_of`: each query has exactly 8 pairs.
All inputs are finite; a program needn't handle non-finite values.
Results may differ from a plain program's by a relative error of at most 0.02.
The roundings to bfloat16 on the way count: a program that leaves them out, or rounds other values in their place, can miss the bound.
Values may be sent and summed in bfloat16 or wider, within the bound.
A program may use at most 128 MiB of HBM per device.

v0:
```python
import math

import jax
import jax.numpy as jnp
from jax import lax
from jax.sharding import Mesh
from jax.sharding import PartitionSpec as P

KV_HEADS = 2
HEAD_DIM = 128
HEADS = 8
QUERY_DP = 2
TENSOR = ("tensor_0", "tensor_1")
DP_TENSOR = ("dp", "tensor_0", "tensor_1")


theta_base = 1000000.0
norm_eps = 1e-06


def gather_axes(x, axes, dim):
    for axis in reversed(axes):
        x = lax.all_gather(x, axis, axis=dim, tiled=True)
    return x


def copy_for_each(x, axis):
    copies = jnp.broadcast_to(x, (lax.axis_size(axis), *x.shape))
    return lax.all_to_all(copies, axis, split_axis=0, concat_axis=0, tiled=True)


def taken_together(x, axis):
    return copy_for_each(x, axis).sum(axis=0)


def rms_scale(values, gain_vector):
    floats = values.astype(jnp.float32)
    return (
        floats
        * lax.rsqrt(jnp.mean(floats * floats, axis=-1, keepdims=True) + norm_eps)
        * gain_vector
    )


def frequency_table(head_dim):
    return theta_base ** (-2.0 * jnp.arange(head_dim // 2, dtype=jnp.float32) / head_dim)


def rotate(values, cosine_table, sine_table):
    half_dim = values.shape[-1] // 2
    first_half = values[..., :half_dim]
    second_half = values[..., half_dim:]
    return jnp.concatenate(
        [
            first_half * cosine_table - second_half * sine_table,
            second_half * cosine_table + first_half * sine_table,
        ],
        axis=-1,
    )


def on_device(
    arrived,
    destination,
    query_of,
    lengths,
    attn_gain,
    q_weight,
    q_bias,
    k_weight,
    v_weight,
    v_bias,
    o_weight,
    mlp_gain,
    w_gate,
    w_up,
    w_down,
    final_gain,
    score_weight,
):
    group_index = lax.axis_index("dp")
    tensor_index = lax.axis_index(TENSOR)
    tensor_count = lax.axis_size(TENSOR)
    row_blocks = lax.all_to_all(arrived, TENSOR, split_axis=1, concat_axis=0, tiled=True)
    pairs_here = row_blocks.shape[0]
    row_targets = lax.dynamic_slice_in_dim(destination, group_index * pairs_here, pairs_here)
    local_order = jnp.argsort(row_targets * pairs_here + jnp.arange(pairs_here, dtype=jnp.int32))
    sorted_rows = jnp.transpose(jnp.take(row_blocks, local_order, axis=0), (1, 0, 2))
    resident = lax.all_to_all(sorted_rows, "dp", split_axis=1, concat_axis=1, tiled=True)
    total_pairs = destination.shape[0]
    global_order = jnp.argsort(destination * total_pairs + jnp.arange(total_pairs, dtype=jnp.int32))
    my_pairs = lax.dynamic_slice_in_dim(global_order, group_index * pairs_here, pairs_here)
    my_lengths = jnp.take(lengths, my_pairs)
    my_queries = jnp.take(query_of, my_pairs)
    seq_local = resident.shape[0]
    seq_len = seq_local * tensor_count
    heads_here = q_weight.shape[1] // HEAD_DIM
    kv_head = tensor_index * heads_here // (HEADS // KV_HEADS)
    key_cols = lax.dynamic_slice_in_dim(k_weight, kv_head * HEAD_DIM, HEAD_DIM, 1)
    value_cols = lax.dynamic_slice_in_dim(v_weight, kv_head * HEAD_DIM, HEAD_DIM, 1)
    value_shift = lax.dynamic_slice_in_dim(v_bias, kv_head * HEAD_DIM, HEAD_DIM)
    joint_weight = jnp.concatenate([q_weight, key_cols, value_cols], axis=1)
    joint_bias = jnp.concatenate(
        [
            q_bias.astype(jnp.float32),
            jnp.zeros((HEAD_DIM,), jnp.float32),
            value_shift.astype(jnp.float32),
        ]
    )
    frequencies = frequency_table(HEAD_DIM)
    query_width = heads_here * HEAD_DIM
    normed = rms_scale(resident, attn_gain).astype(jnp.bfloat16)
    piece_rows = lax.all_gather(normed, TENSOR, axis=0, tiled=True)
    row_total = piece_rows.shape[0]
    projected_rows = (
        jnp.einsum("spd,de->spe", piece_rows, joint_weight, preferred_element_type=jnp.float32)
        + joint_bias
    )
    angles = (
        jnp.arange(row_total, dtype=jnp.int32).astype(jnp.float32)[:, None] * frequencies[None, :]
    )
    cosine_table = jnp.cos(angles)[:, None, None, :]
    sine_table = jnp.sin(angles)[:, None, None, :]
    query_rows = projected_rows[..., :query_width].reshape(
        row_total, pairs_here, heads_here, HEAD_DIM
    )
    key_rows = projected_rows[..., query_width : query_width + HEAD_DIM].reshape(
        row_total, pairs_here, 1, HEAD_DIM
    )
    value_rows = projected_rows[..., query_width + HEAD_DIM :]
    query_rows = rotate(query_rows, cosine_table, sine_table).reshape(
        row_total, pairs_here, query_width
    )
    key_rows = rotate(key_rows, cosine_table, sine_table).reshape(row_total, pairs_here, HEAD_DIM)
    projected = jnp.concatenate([query_rows, key_rows, value_rows], axis=-1).astype(jnp.bfloat16)
    query_all = projected[..., :query_width].reshape(seq_len, pairs_here, heads_here, HEAD_DIM)
    key_all = projected[..., query_width : query_width + HEAD_DIM]
    value_all = projected[..., query_width + HEAD_DIM :]
    logits = jnp.einsum(
        "qphe,kpe->phqk", query_all, key_all, preferred_element_type=jnp.float32
    ) / math.sqrt(HEAD_DIM)
    positions = jnp.arange(seq_len, dtype=jnp.int32)
    allowed = (positions[None, :] <= positions[:, None])[None, :, :] & (
        positions[None, None, :] < my_lengths[:, None, None]
    )
    logits = jnp.where(allowed[:, None, :, :], logits, -1e30)
    shifted = jnp.exp(logits - jnp.max(logits, axis=-1, keepdims=True))
    probs = (shifted / jnp.sum(shifted, axis=-1, keepdims=True)).astype(jnp.bfloat16)
    context = jnp.einsum(
        "phqk,kpe->qphe", probs, value_all, preferred_element_type=jnp.float32
    ).astype(jnp.bfloat16)
    context = context.reshape(seq_len, pairs_here, query_width)
    own_context = lax.all_to_all(context, TENSOR, split_axis=0, concat_axis=2, tiled=True)
    attended = jnp.einsum(
        "spe,ed->spd",
        own_context,
        gather_axes(o_weight, TENSOR, 0),
        preferred_element_type=jnp.float32,
    )
    after_attention = (resident.astype(jnp.float32) + attended).astype(jnp.bfloat16)
    normed_mlp = rms_scale(after_attention, mlp_gain).astype(jnp.bfloat16)
    piece_rows = lax.all_gather(normed_mlp, TENSOR, axis=0, tiled=True)
    gate_values = jnp.einsum("spd,df->spf", piece_rows, w_gate, preferred_element_type=jnp.float32)
    up_values = jnp.einsum("spd,df->spf", piece_rows, w_up, preferred_element_type=jnp.float32)
    activated = (jax.nn.silu(gate_values) * up_values).astype(jnp.bfloat16)
    mlp_sum = lax.psum_scatter(
        jnp.einsum("spf,fd->spd", activated, w_down, preferred_element_type=jnp.float32).astype(
            jnp.bfloat16
        ),
        TENSOR,
        scatter_dimension=0,
        tiled=True,
    ).astype(jnp.float32)
    hidden_out = (after_attention.astype(jnp.float32) + mlp_sum).astype(jnp.bfloat16)
    local_positions = tensor_index * seq_local + jnp.arange(seq_local, dtype=jnp.int32)
    is_last = (local_positions[:, None] == (my_lengths - 1)[None, :]).astype(jnp.bfloat16)
    last_rows = jnp.einsum("sp,spd->pd", is_last, hidden_out, preferred_element_type=jnp.float32)
    partial_score = jnp.sum(rms_scale(last_rows, final_gain) * score_weight, axis=-1)
    pair_score = taken_together(partial_score, TENSOR)
    query_total = lax.axis_size("dp") * QUERY_DP
    membership = (my_queries[:, None] == jnp.arange(query_total, dtype=jnp.int32)[None, :]).astype(
        jnp.float32
    )
    totals = taken_together(jnp.dot(pair_score, membership), "dp")
    mean_all = totals / (total_pairs // query_total)
    centred = pair_score - jnp.dot(membership, mean_all)
    query_mean = lax.dynamic_slice_in_dim(mean_all, group_index * QUERY_DP, QUERY_DP)
    return (hidden_out, centred, query_mean)


def solution(mesh):
    split = Mesh(mesh.devices.reshape(mesh.shape["dp"], 4, 2), ("dp", "tensor_0", "tensor_1"))
    placed = (
        P(DP_TENSOR, None, None),
        P(),
        P(),
        P(),
        P(),
        P(None, TENSOR),
        P(TENSOR),
        P(),
        P(),
        P(),
        P(TENSOR, None),
        P(),
        P(None, TENSOR),
        P(None, TENSOR),
        P(TENSOR, None),
        P(),
        P(),
    )
    return jax.shard_map(
        on_device,
        mesh=split,
        in_specs=placed,
        out_specs=(P(TENSOR, "dp", None), P("dp"), P("dp")),
        check_vma=False,
    )
```

profile of v0, /device:TPU:1, one launch (start us, length us, event | category | flops | bytes accessed | tf_op | source)
XLA Modules:
  0.0 443.9 jit_solution(2030019210064797637)
XLA Ops:
  7.2 3.0 copy.56
  10.2 8.3 %all-to-all-start = ((bf16[2,128,1536]{2,0,1:T(2,128)(2,1)}), bf16[2,128,1536]{2,0,1:T(2,128)(2,1)}, u32[]{:S(2)}, u32[]{:S(2)}) async-start(bf16[2,128,1536]{2,0,1:T(2,128)(2,1)} %copy.56), calls=%async_computation | async-start | bytes 1572864 | tf_op jit(solution)/shard_map/all_to_all | solution.py:84
  21.2 3.2 sort.35
  24.5 7.3 %all-to-all-done = bf16[2,128,1536]{2,0,1:T(2,128)(2,1)} async-done(((bf16[2,128,1536]{2,0,1:T(2,128)(2,1)}), bf16[2,128,1536]{2,0,1:T(2,128)(2,1)}, u32[]{:S(2)}, u32[]{:S(2)}) %all-to-all-start) | async-done | bytes 786464 | tf_op jit(solution)/shard_map/all_to_all | solution.py:84
  34.0 2.6 gather_fusion
  37.9 19.4 %all_to_all.53 = bf16[16,16,1536]{2,0,1:T(8,128)(2,1)S(1)} all-to-all(bf16[16,16,1536]{2,0,1:T(8,128)(2,1)S(1)} %select_bitcast_fusion), channel_id=1, replica_groups=mesh['dp'=16,'tensor_0'=4,'tensor_1'=2] {'dp'}, dimensions={1} | all-to-all | bytes 1572864 | tf_op jit(solution)/shard_map/all_to_all | solution.py:89
  59.3 13.9 %all_gather.13 = bf16[256,1536]{1,0:T(8,128)(2,1)} all-gather(bf16[128,1536]{1,0:T(8,128)(2,1)} %param.29), channel_id=1, replica_groups=mesh['dp'=16,'tensor_0'=4,'tensor_1'=2] {'tensor_1'}, dimensions={0}, use_global_device_ids=true | all-gather | bytes 1179648 | tf_op jit(solution)/shard_map/all_gather | solution.py:23
  75.9 2.1 constant_dynamic-slice_fusion
  77.9 66.0 %all-gather.4.cloned.1.call-done = bf16[128,16,1536]{2,0,1:T(8,128)(2,1)} async-done(((bf16[16,16,1536]{2,0,1:T(8,128)(2,1)}), bf16[128,16,1536]{2,0,1:T(8,128)(2,1)}) %all-gather.4.cloned.1.call-update) | async-done | bytes 6291472 | tf_op jit(solution)/shard_map/all_gather | solution.py:113
  144.0 5.9 %convolution_add_fusion = f32[128,16,384]{2,0,1:T(8,128)S(1)} fusion(bf16[128,16,1536]{2,0,1:T(8,128)(2,1)} %all-gather.4.cloned.1.call-done, f32[384]{0:T(512)S(1)} %pad_maximum_fusion, bf16[1536,128]{1,0:T(8,128)(2,1)} %get-tuple-element.45, bf16[1536,128]{1,0:T(8,128)(2,1)} %get-tuple-element.46, bf16[1536,128]{1,0:T(8,128)(2,1)} %param.24), kind=kOutput, calls=%fused_computation.16 | convolution fusion | flops 2420244480 | bytes 10618368 | tf_op jit(solution)/shard_map/spd,de->spe/dot_general | solution.py:116
  153.7 2.3 copy.61
  156.0 15.4 %all_to_all.54 = bf16[128,16,128]{2,1,0:T(8,128)(2,1)S(1)} all-to-all(bf16[128,16,128]{2,1,0:T(8,128)(2,1)} %copy.61), channel_id=1, replica_groups=mesh['dp'=16,'tensor_0'=4,'tensor_1'=2] {'tensor_0','tensor_1'}, dimensions={0} | all-to-all | bytes 1048576 | tf_op jit(solution)/shard_map/all_to_all | solution.py:153
  172.6 2.1 reshape.241
  174.7 14.6 %all-gather.6.cloned.1.call-done = bf16[1024,1536]{1,0:T(8,128)(2,1)} async-done(((bf16[256,1536]{1,0:T(8,128)(2,1)}), bf16[1024,1536]{1,0:T(8,128)(2,1)}) %all-gather.6.cloned.1.call-update) | async-done | bytes 3145744 | tf_op jit(solution)/shard_map/all_gather | solution.py:23
  189.3 3.3 multiply_reduce_fusion
  195.1 88.1 %all-gather.8.cloned.1.call-done = bf16[128,16,1536]{2,0,1:T(8,128)(2,1)} async-done(((bf16[16,16,1536]{2,0,1:T(8,128)(2,1)}), bf16[128,16,1536]{2,0,1:T(8,128)(2,1)}) %all-gather.8.cloned.1.call-update) | async-done | bytes 6291472 | tf_op jit(solution)/shard_map/all_gather | solution.py:162
  283.2 10.6 %fusion.1 = f32[128,16,1120]{0,2,1:T(8,128)S(1)} fusion(bf16[128,16,1536]{2,0,1:T(8,128)(2,1)} %all-gather.8.cloned.1.call-done, bf16[1536,1120]{0,1:T(8,128)(2,1)} %param.32), kind=kOutput, calls=%fused_computation.6 | convolution fusion | flops 7046430720 | bytes 18907136 | tf_op jit(solution)/shard_map/spd,df->spf/dot_general | solution.py:164
  293.9 8.7 %multiply_convert_fusion = bf16[128,16,1120]{0,2,1:T(8,128)(2,1)S(1)} fusion(f32[128,16,1120]{0,2,1:T(8,128)S(1)} %fusion.1, bf16[128,16,1536]{2,0,1:T(8,128)(2,1)S(1)} %copy-done.11, bf16[1536,1120]{0,1:T(8,128)(2,1)S(1)} %copy-done.12), kind=kOutput, calls=%fused_computation.3 | convolution fusion | flops 7060193280 | bytes 23494656 | tf_op jit(solution)/shard_map/spd,df->spf/dot_general | solution.py:163
  302.6 10.3 %convolution_convert_fusion = bf16[128,16,1536]{2,0,1:T(8,128)(2,1)} fusion(bf16[128,16,1120]{0,2,1:T(8,128)(2,1)S(1)} %multiply_convert_fusion, bf16[1120,1536]{1,0:T(8,128)(2,1)S(1)} %copy-done), kind=kOutput, calls=%fused_computation.4 | convolution fusion | flops 7049576448 | bytes 14319616 | tf_op jit(solution)/shard_map/spf,fd->spd/dot_general | solution.py:167
  313.1 95.8 %reduce-scatter.2.cloned.1.call-done = bf16[16,16,1536]{2,0,1:T(8,128)(2,1)} async-done(((bf16[128,16,1536]{2,0,1:T(8,128)(2,1)}), bf16[16,16,1536]{2,0,1:T(8,128)(2,1)}) %reduce-scatter.2.cloned.1.call-update) | async-done | bytes 786448 | tf_op jit(solution)/shard_map/reduce_scatter | solution.py:166
  412.2 8.9 %all_to_all.55 = f32[8,1,16]{2,1,0:T(1,128)S(1)} all-to-all(f32[8,1,16]{2,1,0:T(1,128)S(1)} %broadcast_in_dim.30), channel_id=1, replica_groups=mesh['dp'=16,'tensor_0'=4,'tensor_1'=2] {'tensor_0','tensor_1'}, dimensions={0} | all-to-all | bytes 1024 | tf_op jit(solution)/shard_map/all_to_all | solution.py:29
  421.9 8.7 %all-to-all-start.4 = ((f32[16,1,32]{2,1,0:T(1,128)}), f32[16,1,32]{2,1,0:T(1,128)S(1)}, u32[]{:S(2)}, u32[]{:S(2)}) async-start(f32[16,1,32]{2,1,0:T(1,128)} %broadcast_in_dim.31), calls=%async_computation.5 | async-start | bytes 16384 | tf_op jit(solution)/shard_map/all_to_all | solution.py:29
  430.6 2.4 copy.66
  433.0 3.1 all-to-all-done.4
  (89 shorter events, 23.9 us)
Async XLA Ops:
  7.2 295.4 %copy-start = (bf16[1120,1536]{1,0:T(8,128)(2,1)S(1)}, bf16[1120,1536]{1,0:T(8,128)(2,1)}, u32[]{:S(2)}) copy-start(bf16[1120,1536]{1,0:T(8,128)(2,1)} %param.33) | copy-start | bytes 10321924
  10.2 21.7 %all-to-all-start = ((bf16[2,128,1536]{2,0,1:T(2,128)(2,1)}), bf16[2,128,1536]{2,0,1:T(2,128)(2,1)}, u32[]{:S(2)}, u32[]{:S(2)}) async-start(bf16[2,128,1536]{2,0,1:T(2,128)(2,1)} %copy.56), calls=%async_computation | async-start | bytes 1572864 | tf_op jit(solution)/shard_map/all_to_all | solution.py:84
  18.5 125.5 %all-gather.4.cloned.1.call-start = ((), (), s32[]{:S(2)}) async-start(), calls=%async_computation.6 | async-start | bytes 7077888 | tf_op jit(solution)/shard_map/all_gather | solution.py:113
  33.0 25.1 %copy-start.7 = (f32[1536]{0:T(1024)S(1)}, f32[1536]{0:T(1024)}, u32[]{:S(2)}) copy-start(f32[1536]{0:T(1024)} %param.23) | copy-start | bytes 18436
  37.9 35.5 %copy-start.13 = (bf16[128]{0:T(256)(128)(2,1)S(1)}, bf16[128]{0:T(256)(128)(2,1)}, u32[]{:S(2)}) copy-start(bf16[128]{0:T(256)(128)(2,1)} %param.25) | copy-start | bytes 772
  37.9 35.5 %copy-start.1 = (s32[256]{0:T(256)S(1)}, s32[256]{0:T(256)}, u32[]{:S(2)}) copy-start(s32[256]{0:T(256)} %param.22) | copy-start | bytes 3076
  37.9 36.2 %copy-start.2 = (s32[256]{0:T(256)S(1)}, s32[256]{0:T(256)}, u32[]{:S(2)}) copy-start(s32[256]{0:T(256)} %param.21) | copy-start | bytes 3076
  57.2 0.9 copy-start.3
  57.2 17.5 %copy-start.14 = (bf16[256]{0:T(256)(128)(2,1)S(1)}, bf16[256]{0:T(256)(128)(2,1)}, u32[]{:S(2)}) copy-start(bf16[256]{0:T(256)(128)(2,1)} %param.28) | copy-start | bytes 1540
  59.3 130.0 %all-gather.6.cloned.1.call-start = ((), (), s32[]{:S(2)}) async-start(), calls=%async_computation.7 | async-start | bytes 3932160 | tf_op jit(solution)/shard_map/all_gather | solution.py:23
  73.3 210.0 %all-gather.8.cloned.1.call-start = ((), (), s32[]{:S(2)}) async-start(), calls=%async_computation.8 | async-start | bytes 7077888 | tf_op jit(solution)/shard_map/all_gather | solution.py:162
  149.8 0.8 copy-start.6
  172.6 21.2 %copy-start.8 = (f32[1536]{0:T(1024)S(1)}, f32[1536]{0:T(1024)}, u32[]{:S(2)}) copy-start(f32[1536]{0:T(1024)} %param.30) | copy-start | bytes 18436
  192.6 1.1 copy-start.5
  194.9 214.0 %reduce-scatter.2.cloned.1.call-start = ((), (), s32[]{:S(2)}) async-start(), calls=%async_computation.9 | async-start | bytes 7077888 | tf_op jit(solution)/shard_map/reduce_scatter | solution.py:166
  283.2 10.6 %copy-start.11 = (bf16[128,16,1536]{2,0,1:T(8,128)(2,1)S(1)}, bf16[128,16,1536]{2,0,1:T(8,128)(2,1)}, u32[]{:S(2)}) copy-start(bf16[128,16,1536]{2,0,1:T(8,128)(2,1)} %all-gather.8.cloned.1.call-done) | copy-start | bytes 18874372
  283.2 10.6 %copy-start.12 = (bf16[1536,1120]{0,1:T(8,128)(2,1)S(1)}, bf16[1536,1120]{0,1:T(8,128)(2,1)}, u32[]{:S(2)}) copy-start(bf16[1536,1120]{0,1:T(8,128)(2,1)} %param.31) | copy-start | bytes 10321924
  312.9 99.1 %copy-start.9 = (f32[1536]{0:T(1024)S(1)}, f32[1536]{0:T(1024)}, u32[]{:S(2)}) copy-start(f32[1536]{0:T(1024)} %param.35) | copy-start | bytes 18436
  312.9 99.1 %copy-start.10 = (f32[1536]{0:T(1024)S(1)}, f32[1536]{0:T(1024)}, u32[]{:S(2)}) copy-start(f32[1536]{0:T(1024)} %param.34) | copy-start | bytes 18436
  410.7 0.9 copy-start.4
  421.9 14.2 %all-to-all-start.4 = ((f32[16,1,32]{2,1,0:T(1,128)}), f32[16,1,32]{2,1,0:T(1,128)S(1)}, u32[]{:S(2)}, u32[]{:S(2)}) async-start(f32[16,1,32]{2,1,0:T(1,128)} %broadcast_in_dim.31), calls=%async_computation.5 | async-start | bytes 16384 | tf_op jit(solution)/shard_map/all_to_all | solution.py:29
Sparse Core Ops, SparseCore 0:
  59.4 84.5 all-gather.3
  145.6 43.6 all-gather.5
  195.0 88.1 all-gather.7
  313.0 95.8 reduce-scatter.1
where the time goes:
time: 445 us; the launch traced here: 444 us
  waiting for transfers between devices  275 us (62%)
  blocking collectives  57.6 us (13%)
  matrix products  42 us (9%)
  local copies, waits for them, and re-layouts  23.9 us (5%)
  starting transfers between devices  17.3 us (4%)
  between operations  14.1 us (3%)
  other arithmetic  14 us (3%)
    reduce_scatter x1, waiting for transfers between devices, on_device(): lax.psum_scatter(jnp.einsum('spf,fd->spd', activated, w_down, preferred_e...  95.8 us
    all_gather x1, waiting for transfers between devices, on_device(): piece_rows = lax.all_gather(normed_mlp, TENSOR, axis=0, tiled=True)  88.1 us
    all_gather x1, waiting for transfers between devices, on_device(): piece_rows = lax.all_gather(normed, TENSOR, axis=0, tiled=True)  66 us
    all_to_all x1, blocking collectives, on_device(): lax.all_to_all(sorted_rows, 'dp', split_axis=1, concat_axis=1, tiled=True)  19.4 us
    all_to_all x1, blocking collectives, on_device(): lax.all_to_all(context, TENSOR, split_axis=0, concat_axis=2, tiled=True)  15.4 us
    all_gather x1, waiting for transfers between devices, gather_axes(): x = lax.all_gather(x, axis, axis=dim, tiled=True)  14.6 us
    all_gather x1, blocking collectives, gather_axes(): x = lax.all_gather(x, axis, axis=dim, tiled=True)  13.9 us
    dot_general x1, matrix products, on_device(): jnp.einsum('spd,df->spf', piece_rows, w_up, preferred_element_type=jnp.fl...  10.6 us
  transfers between devices with their start and end apart: 6, of which 6 were waited for; matrix products, arithmetic and copies ran while one was open for 6% of the time, Pallas kernels for 0%

commit v1 on v0

v1 whole, which is shorter than its diff:
```python
import functools
import math

import jax
import jax.numpy as jnp
import numpy as np
from jax import lax
from jax.experimental import pallas as pl
from jax.experimental.pallas import tpu as pltpu
from jax.sharding import Mesh
from jax.sharding import PartitionSpec as P

AXES = ("y", "xl", "c", "z", "xh")
DP = ("y", "xl", "c")
TENSOR = ("z", "xh")
MESH = pl.DeviceIdType.MESH
F32 = jnp.float32
BF16 = jnp.bfloat16

KV_HEADS = 2
HEAD_DIM = 128
HEADS = 8
QUERY_DP = 2
theta_base = 1000000.0
norm_eps = 1e-06

SEQ = 128
D = 1536
FFL = 1120
FULL = 1024
TAIL = FFL - FULL
FFP = 1152

C1 = (0, 144)
C1A, C1B = (0, 80), (80, 144)
C2 = (144, 256)
C2A, C2B = (144, 208), (208, 256)
N1, N1A = 9, 5
N2A = 13


def z_at(step):
    return lax.rem(lax.axis_index("z") + step + 4, 4)


class Sender:
    def __init__(self, send_sem, recv_sem):
        self.send_sem, self.recv_sem, self.count = send_sem, recv_sem, 0
        self.open = []

    def __call__(self, src, dst, device):
        i = self.count
        self.count += 1
        copy = pltpu.make_async_remote_copy(
            src_ref=src,
            dst_ref=dst,
            send_sem=self.send_sem.at[i],
            recv_sem=self.recv_sem.at[i],
            device_id=device,
            device_id_type=MESH,
        )
        copy.start()
        self.open.append(copy)
        return copy

    def drain(self):
        for copy in self.open:
            copy.wait_send()
        self.open = []


def tensor_peer(k):
    index = lax.rem(lax.axis_index("z") * 2 + lax.axis_index("xh") + k, 8)
    return {"z": index // 2, "xh": lax.rem(index, 2)}


def dp_peer(k):
    index = lax.axis_index("y") * 4 + lax.axis_index("xl") * 2 + lax.axis_index("c")
    index = lax.rem(index + k, 16)
    return index, {"y": index // 4, "xl": lax.rem(index // 2, 2), "c": lax.rem(index, 2)}


def greet(devices):
    barrier = pltpu.get_barrier_semaphore()
    for device in devices:
        pl.semaphore_signal(barrier, inc=1, device_id=device, device_id_type=MESH)
    pl.semaphore_wait(barrier, len(devices))


def rms_rows(values, gain):
    scale = lax.rsqrt(jnp.mean(values * values, axis=-1, keepdims=True) + norm_eps)
    return values * scale * gain


def rotate(values, cosine, sine):
    return values * cosine + pltpu.roll(values, HEAD_DIM // 2, 1) * sine


def attention_kernel(
    lengths, gain, mlp_gain, q_bias, v_bias, cosine, sine, arrived, q_w, k_w, v_w, o_w,
    after_out, normed_out,
    x_v, k_v, v_v, q_all, o_all, bias_one, bias_all, normed, keys, values, queries, context,
    local_sem, send_sem, recv_sem,
):
    z, xh, c = lax.axis_index("z"), lax.axis_index("xh"), lax.axis_index("c")
    y, xl = lax.axis_index("y"), lax.axis_index("xl")
    t = z * 2 + xh
    partner, sibling = {"xh": 1 - xh}, {"c": 1 - c}
    up, down = {"z": z_at(1)}, {"z": z_at(-1)}

    def q_cols(index):
        return pl.ds(pl.multiple_of(index * HEAD_DIM, HEAD_DIM), HEAD_DIM)

    loads = [
        pltpu.make_async_copy(arrived, x_v, local_sem.at[0]),
        pltpu.make_async_copy(k_w, k_v, local_sem.at[1]),
        pltpu.make_async_copy(v_w, v_v, local_sem.at[2]),
        pltpu.make_async_copy(q_w, q_all.at[:, q_cols(t)], local_sem.at[3]),
        pltpu.make_async_copy(
            o_w, o_all.at[pl.ds(pl.multiple_of(t * HEAD_DIM, HEAD_DIM), HEAD_DIM)], local_sem.at[4]
        ),
    ]
    for load in loads:
        load.start()
    bias_one[...] = jnp.broadcast_to(q_bias[...].astype(F32), bias_one.shape)
    greet([tensor_peer(k) for k in range(1, 8)] + [sibling])
    send = Sender(send_sem, recv_sem)

    half_q, half_o = D // 2, HEAD_DIM // 2

    def q_piece(index, sub=None):
        size = half_q if sub is None else half_q // 2
        start = c * half_q + (0 if sub is None else sub * size)
        return q_all.at[pl.ds(pl.multiple_of(start, 128), size), q_cols(index)]

    def o_piece(index, sub=None):
        size = half_o if sub is None else half_o // 2
        start = index * HEAD_DIM + c * half_o + (0 if sub is None else sub * size)
        return o_all.at[pl.ds(pl.multiple_of(start, 32), size)]

    zp, zm, z2 = z_at(1), z_at(-1), z_at(2)
    own_q = q_w.at[pl.ds(pl.multiple_of(c * half_q, 128), half_q)]
    own_o = o_w.at[pl.ds(pl.multiple_of(c * half_o, 64), half_o)]

    def first(piece, own):
        return [send(own, piece(t), partner), send(own, piece(t), up), send(own, piece(t), down)]

    q_x, q_u, q_d = first(q_piece, own_q)
    bias_copies = [send(bias_one, bias_all.at[t], tensor_peer(k)) for k in range(1, 8)]
    o_x, o_u, o_d = first(o_piece, own_o)

    loads[0].wait()
    x = x_v[...].reshape(2 * SEQ, D)
    normed[...] = rms_rows(x.astype(F32), gain[...]).astype(BF16)
    loads[1].wait()
    loads[2].wait()
    cos_rows = jnp.concatenate([cosine[...]] * 2, axis=0)
    sin_rows = jnp.concatenate([sine[...]] * 2, axis=0)
    k_f = jnp.dot(normed[...], k_v[...], preferred_element_type=F32)
    for g in range(KV_HEADS):
        cols = slice(g * HEAD_DIM, (g + 1) * HEAD_DIM)
        keys[:, cols] = rotate(k_f[:, cols], cos_rows, sin_rows).astype(BF16)
    v_f = jnp.dot(normed[...], v_v[...], preferred_element_type=F32)
    values[...] = (v_f + v_bias[...].astype(F32)).astype(BF16)

    def second(piece, x_c, u_c, d_c):
        x_c.wait_recv()
        other = z * 2 + 1 - xh
        a = send(piece(other), piece(other), up)
        b = send(piece(other), piece(other), down)
        s = [send(piece(other), piece(other), sibling)]
        u_c.wait_recv()
        low, high = zm * 2 + xh, zp * 2 + xh
        f = send(piece(low, 0), piece(low, 0), up)
        s.append(send(piece(low), piece(low), sibling))
        d_c.wait_recv()
        h = send(piece(high, 1), piece(high, 1), down)
        s.append(send(piece(high), piece(high), sibling))
        return a, b, f, h, s

    def third(piece, a, b, f, h, s):
        low, high, far = zm * 2 + 1 - xh, zp * 2 + 1 - xh, z2 * 2 + 1 - xh
        mine = z2 * 2 + xh
        a.wait_recv()
        f2 = send(piece(low, 0), piece(low, 0), up)
        s.append(send(piece(low), piece(low), sibling))
        b.wait_recv()
        h2 = send(piece(high, 1), piece(high, 1), down)
        s.append(send(piece(high), piece(high), sibling))
        f.wait_recv()
        s.append(send(piece(mine, 0), piece(mine, 0), sibling))
        h.wait_recv()
        s.append(send(piece(mine, 1), piece(mine, 1), sibling))
        return f2, h2, far

    def fourth(piece, f2, h2, far, s):
        f2.wait_recv()
        s.append(send(piece(far, 0), piece(far, 0), sibling))
        h2.wait_recv()
        s.append(send(piece(far, 1), piece(far, 1), sibling))

    q_state = second(q_piece, q_x, q_u, q_d)
    o_state = second(o_piece, o_x, o_u, o_d)
    q_last = third(q_piece, *q_state)
    o_last = third(o_piece, *o_state)
    fourth(q_piece, *q_last, q_state[4])
    for copy in q_state[4]:
        copy.wait_recv()
    loads[3].wait()
    for copy in bias_copies:
        copy.wait_recv()
    bias_all[t] = bias_one[...]

    def project(i, carry):
        cols = pl.ds(pl.multiple_of(i * 256, 256), 256)
        q_f = jnp.dot(normed[...], q_all[:, cols], preferred_element_type=F32)
        for e in range(2):
            q_e = q_f[:, e * HEAD_DIM : (e + 1) * HEAD_DIM] + bias_all[2 * i + e][0:1]
            at = pl.ds(pl.multiple_of(i * 256 + e * HEAD_DIM, HEAD_DIM), HEAD_DIM)
            queries[:, at] = rotate(q_e, cos_rows, sin_rows).astype(BF16)
        return carry

    lax.fori_loop(0, HEADS // 2, project, 0)

    q_pos = lax.broadcasted_iota(jnp.int32, (SEQ, SEQ), 0)
    k_pos = lax.broadcasted_iota(jnp.int32, (SEQ, SEQ), 1)
    group = HEADS // KV_HEADS
    first_pair = ((y * 4 + xl * 2 + c) * 8 + t) * 2
    for p in range(2):
        rows = slice(p * SEQ, (p + 1) * SEQ)
        allowed = (k_pos <= q_pos) & (k_pos < lengths[first_pair + p])
        allowed = jnp.concatenate([allowed.astype(F32)] * group, axis=0) > 0.5
        for g in range(KV_HEADS):
            cols = slice(g * HEAD_DIM, (g + 1) * HEAD_DIM)
            q_g = jnp.concatenate(
                [
                    queries[rows, (g * group + h) * HEAD_DIM : (g * group + h + 1) * HEAD_DIM]
                    for h in range(group)
                ],
                axis=0,
            )
            logits = lax.dot_general(
                q_g, keys[rows, cols], (((1,), (1,)), ((), ())), preferred_element_type=F32
            ) / math.sqrt(HEAD_DIM)
            logits = jnp.where(allowed, logits, -1e30)
            shifted = jnp.exp(logits - jnp.max(logits, axis=-1, keepdims=True))
            probs = (shifted / jnp.sum(shifted, axis=-1, keepdims=True)).astype(BF16)
            ctx = jnp.dot(probs, values[rows, cols], preferred_element_type=F32).astype(BF16)
            for h in range(group):
                at = (g * group + h) * HEAD_DIM
                context[rows, at : at + HEAD_DIM] = ctx[h * SEQ : (h + 1) * SEQ]

    fourth(o_piece, *o_last, o_state[4])
    for copy in o_state[4]:
        copy.wait_recv()
    loads[4].wait()

    def project_out(i, carry):
        cols = pl.ds(pl.multiple_of(i * 256, 256), 256)
        attended = jnp.dot(context[...], o_all[:, cols], preferred_element_type=F32)
        base = x_v[:, :, cols].reshape(2 * SEQ, 256).astype(F32)
        after_out[:, cols] = (base + attended).astype(BF16)
        return carry

    lax.fori_loop(0, D // 256, project_out, 0)
    normed_out[...] = rms_rows(after_out[...].astype(F32), mlp_gain[...]).astype(BF16)
    send.drain()


def mlp_kernel(
    lengths, destination, final_gain, score_weight, normed, after, w_gate, w_up, w_down,
    relaid_out, scores_out,
    gathered, after_v, wg, wu, wd, w_tail, active, partial,
    r1_low, r1_high, r1_up, r1_down, r1_x, r2_x, r2_low, r2_high, r2_up, r2_down,
    staged, landed, last_rows, score_one, score_eight, score_sum, score_all,
    local_sem, send_sem, recv_sem,
):
    z, xh, c = lax.axis_index("z"), lax.axis_index("xh"), lax.axis_index("c")
    y, xl = lax.axis_index("y"), lax.axis_index("xl")
    t = z * 2 + xh
    b = y * 4 + xl * 2 + c
    partner = {"xh": 1 - xh}
    up, down = {"z": z_at(1)}, {"z": z_at(-1)}
    zp, zm, z2 = z_at(1), z_at(-1), z_at(2)

    loads = [
        pltpu.make_async_copy(normed, gathered.at[t], local_sem.at[0]),
        pltpu.make_async_copy(w_gate, wg, local_sem.at[1]),
        pltpu.make_async_copy(w_up, wu, local_sem.at[2]),
        pltpu.make_async_copy(w_down, wd.at[pl.ds(0, FFL)], local_sem.at[3]),
        pltpu.make_async_copy(after, after_v, local_sem.at[4]),
    ]
    for load in loads:
        load.start()
    greet([tensor_peer(k) for k in range(1, 8)] + [dp_peer(k)[1] for k in range(1, 16)])
    send = Sender(send_sem, recv_sem)

    def rows(g, span):
        return gathered.at[g, pl.ds(span[0], span[1] - span[0])]

    def pass_on(g, span, device):
        return send(rows(g, span), rows(g, span), device)

    here, there = t, z * 2 + 1 - xh
    low, high = zm * 2 + xh, zp * 2 + xh
    low_x, high_x = zm * 2 + 1 - xh, zp * 2 + 1 - xh
    far, far_x = z2 * 2 + xh, z2 * 2 + 1 - xh

    loads[0].wait()
    u2 = pass_on(here, C2, up)
    d2 = pass_on(here, C2, down)
    x1 = pass_on(here, C1, partner)
    u1 = pass_on(here, C1, up)
    d1 = pass_on(here, C1, down)
    x2 = pass_on(here, C2, partner)

    wd[FFL:FFP] = jnp.zeros((FFP - FFL, D), BF16)
    w_tail[...] = jnp.zeros_like(w_tail)
    loads[1].wait()
    w_tail[:, 0:TAIL] = wg[:, FULL:FFL]
    loads[2].wait()
    w_tail[:, 128 : 128 + TAIL] = wu[:, FULL:FFL]
    loads[3].wait()
    loads[4].wait()

    def gated(gate_values, up_values):
        return (gate_values / (1.0 + jnp.exp(-gate_values)) * up_values).astype(BF16)

    def block(g, own=False):
        def hidden(i, carry):
            cols = pl.ds(pl.multiple_of(i * 256, 256), 256)
            gate_values = jnp.dot(gathered[g], wg[:, cols], preferred_element_type=F32)
            up_values = jnp.dot(gathered[g], wu[:, cols], preferred_element_type=F32)
            active[:, cols] = gated(gate_values, up_values)
            return carry

        lax.fori_loop(0, FULL // 256, hidden, 0)
        both = jnp.dot(gathered[g], w_tail[...], preferred_element_type=F32)
        active[:, FULL:FFP] = gated(both[:, :128], both[:, 128:])

        def project(i, carry):
            cols = pl.ds(pl.multiple_of(i * 256, 256), 256)
            result = jnp.dot(active[...], wd[:, cols], preferred_element_type=F32)
            if own:
                result = result.astype(BF16).astype(F32) + after_v[:, cols].astype(F32)
            result = result.astype(BF16).reshape(2, 8, 16, 256)
            for owner in range(8):
                partial[owner, pl.ds(2 * g, 2), :, cols] = result[:, owner]
            return carry

        lax.fori_loop(0, D // 256, project, 0)

    block(here, own=True)
    u2.wait_recv()
    f2u = pass_on(low, C2A, up)
    x_low = pass_on(low, C2, partner)
    d2.wait_recv()
    f2d = pass_on(high, C2B, down)
    x_high = pass_on(high, C2, partner)
    x1.wait_recv()
    xu = pass_on(there, C1, up)
    xd = pass_on(there, C1, down)
    u1.wait_recv()
    f1u = pass_on(low, C1A, up)
    d1.wait_recv()
    f1d = pass_on(high, C1B, down)
    block(low)
    f2u.wait_recv()
    x_far_a = pass_on(far, C2A, partner)
    f2d.wait_recv()
    x_far_b = pass_on(far, C2B, partner)
    block(high)
    x2.wait_recv()
    block(there)
    xu.wait_recv()
    fxu = pass_on(low_x, C1A, up)
    xd.wait_recv()
    fxd = pass_on(high_x, C1B, down)
    x_low.wait_recv()
    block(low_x)
    x_high.wait_recv()
    block(high_x)
    f1u.wait_recv()
    f1d.wait_recv()
    block(far)
    fxu.wait_recv()
    fxd.wait_recv()
    x_far_a.wait_recv()
    x_far_b.wait_recv()
    block(far_x)

    def both_of(zz, lo, hi):
        return partial.at[pl.ds(2 * zz, 2), pl.ds(lo, hi - lo)]

    def one_of(index, lo, hi):
        return partial.at[index, pl.ds(lo, hi - lo)]

    a_up = send(both_of(z2, 0, N1A), r1_low, up)
    a_down = send(both_of(z2, N1A, N1), r1_high, down)
    sx = [
        send(one_of(zz * 2 + 1 - xh, N1, 16), r2_x.at[k], partner)
        for k, zz in enumerate((z2, zp, zm, z))
    ]

    def add_both(zz, lo, extra):
        def step(i, carry):
            for e in range(2):
                index = (2 * zz + e, lo + i)
                partial[index] = (partial[index].astype(F32) + extra[e, i].astype(F32)).astype(BF16)
            return carry

        lax.fori_loop(0, extra.shape[1], step, 0)

    def add_one(index, lo, extra, offset=0):
        def step(i, carry):
            at = (index, lo + i)
            partial[at] = (partial[at].astype(F32) + extra[i].astype(F32)).astype(BF16)
            return carry

        lax.fori_loop(0, extra.shape[0], step, 0)

    a_up.wait_recv()
    add_both(zp, 0, r1_low)
    b_up = send(both_of(zp, 0, N1), r1_up, up)
    a_down.wait_recv()
    add_both(zm, N1A, r1_high)
    b_down = send(both_of(zm, 0, N1), r1_down, down)

    sx[0].wait_recv()
    add_one(z2 * 2 + xh, N1, r2_x.at[0])
    c_up = send(one_of(z2 * 2 + xh, N1, N2A), r2_low, up)
    c_down = send(one_of(z2 * 2 + xh, N2A, 16), r2_high, down)
    sx[1].wait_recv()
    add_one(zp * 2 + xh, N1, r2_x.at[1])
    sx[2].wait_recv()
    add_one(zm * 2 + xh, N1, r2_x.at[2])

    b_up.wait_recv()
    b_down.wait_recv()

    def fold(i, carry):
        at = (z * 2 + 1 - xh, i)
        total = partial[at].astype(F32) + r1_up[1 - xh, i].astype(F32)
        partial[at] = (total + r1_down[1 - xh, i].astype(F32)).astype(BF16)
        return carry

    lax.fori_loop(0, N1, fold, 0)
    ex = send(one_of(z * 2 + 1 - xh, 0, N1), r1_x, partner)

    c_up.wait_recv()
    add_one(zp * 2 + xh, N1, r2_low)
    e_up = send(one_of(zp * 2 + xh, N1, 16), r2_up, up)
    c_down.wait_recv()
    add_one(zm * 2 + xh, N2A, r2_high)
    e_down = send(one_of(zm * 2 + xh, N1, 16), r2_down, down)
    sx[3].wait_recv()
    add_one(t, N1, r2_x.at[3])

    ex.wait_recv()

    def last_one(i, carry):
        total = partial[t, i].astype(F32) + r1_up[xh, i].astype(F32)
        total = total + r1_down[xh, i].astype(F32) + r1_x[i].astype(F32)
        partial[t, i] = total.astype(BF16)
        return carry

    lax.fori_loop(0, N1, last_one, 0)
    e_up.wait_recv()
    e_down.wait_recv()

    def last_two(i, carry):
        total = partial[t, N1 + i].astype(F32) + r2_up[i].astype(F32)
        partial[t, N1 + i] = (total + r2_down[i].astype(F32)).astype(BF16)
        return carry

    lax.fori_loop(0, 16 - N1, last_two, 0)

    pair_copies = []
    for k in range(16):
        index, device = dp_peer(k)
        pair = jnp.int32(0)
        for j in range(1, 16):
            pair = jnp.where(destination[b * 16 + j] == index, j, pair)
        if k == 0:
            landed[b] = partial[t, pair]
        else:
            staged[k] = partial[t, pair]
            pair_copies.append(send(staged.at[k], landed.at[b], device))

    position = lax.broadcasted_iota(jnp.int32, (16, D), 0)
    for p in range(16):
        wanted = lengths[b * 16 + p] - 1 - t * 16
        row = jnp.where(position == wanted, partial[t, p].astype(F32), 0.0)
        last_rows[p : p + 1] = jnp.sum(row, axis=0, keepdims=True)
    scored = rms_rows(last_rows[...], final_gain[...]) * score_weight[...]
    score_one[...] = jnp.broadcast_to(jnp.sum(scored, axis=-1, keepdims=True), score_one.shape)
    copies = [send(score_one, score_eight.at[t], tensor_peer(k)) for k in range(1, 8)]
    score_eight[t] = score_one[...]
    for copy in copies:
        copy.wait_recv()
    total = score_eight[0]
    for k in range(1, 8):
        total = total + score_eight[k]
    score_sum[...] = total
    score_all[b] = total
    copies = [send(score_sum, score_all.at[b], dp_peer(k)[1]) for k in range(1, 16)]
    for copy in copies:
        copy.wait_recv()
    scores_out[...] = score_all[...]
    for copy in pair_copies:
        copy.wait_recv()
    relaid_out[...] = landed[...]
    send.drain()


def any_spec():
    return pl.BlockSpec(memory_space=pl.ANY)


def vmem_spec():
    return pl.BlockSpec(memory_space=pltpu.VMEM)


def smem_spec():
    return pl.BlockSpec(memory_space=pltpu.SMEM)


def rotary_tables():
    index = np.arange(HEAD_DIM // 2, dtype=np.float32)
    frequency = np.power(np.float64(theta_base), -2.0 * index / HEAD_DIM).astype(np.float32)
    angles = np.arange(SEQ, dtype=np.float32)[:, None] * frequency[None, :]
    cosine, sine = np.cos(angles.astype(np.float64)), np.sin(angles.astype(np.float64))
    return (
        np.concatenate([cosine, cosine], axis=1).astype(np.float32),
        np.concatenate([-sine, sine], axis=1).astype(np.float32),
    )


def on_device(
    arrived, destination, query_of, lengths, attn_gain, q_weight, q_bias, k_weight, v_weight,
    v_bias, o_weight, mlp_gain, w_gate, w_up, w_down, final_gain, score_weight,
):
    cosine, sine = rotary_tables()
    row = lambda v: v.reshape(1, -1)
    after, normed = pl.pallas_call(
        attention_kernel,
        out_shape=[jax.ShapeDtypeStruct((2 * SEQ, D), BF16)] * 2,
        in_specs=[smem_spec()] + [vmem_spec()] * 6 + [any_spec()] * 5,
        out_specs=[vmem_spec()] * 2,
        scratch_shapes=[
            pltpu.VMEM((2, SEQ, D), BF16),
            pltpu.VMEM((D, KV_HEADS * HEAD_DIM), BF16),
            pltpu.VMEM((D, KV_HEADS * HEAD_DIM), BF16),
            pltpu.VMEM((D, HEADS * HEAD_DIM), BF16),
            pltpu.VMEM((HEADS * HEAD_DIM, D), BF16),
            pltpu.VMEM((8, HEAD_DIM), F32),
            pltpu.VMEM((8, 8, HEAD_DIM), F32),
            pltpu.VMEM((2 * SEQ, D), BF16),
            pltpu.VMEM((2 * SEQ, KV_HEADS * HEAD_DIM), BF16),
            pltpu.VMEM((2 * SEQ, KV_HEADS * HEAD_DIM), BF16),
            pltpu.VMEM((2 * SEQ, HEADS * HEAD_DIM), BF16),
            pltpu.VMEM((2 * SEQ, HEADS * HEAD_DIM), BF16),
            pltpu.SemaphoreType.DMA((5,)),
            pltpu.SemaphoreType.DMA((48,)),
            pltpu.SemaphoreType.DMA((48,)),
        ],
        compiler_params=pltpu.CompilerParams(
            collective_id=0, has_side_effects=True, vmem_limit_bytes=60 * 2**20
        ),
    )(
        lengths, row(attn_gain), row(mlp_gain), row(q_bias), row(v_bias), cosine, sine,
        arrived, q_weight, k_weight, v_weight, o_weight,
    )
    pairs = lambda *lead: pltpu.VMEM((*lead, 16, D), BF16)
    relaid, scores = pl.pallas_call(
        mlp_kernel,
        out_shape=[
            jax.ShapeDtypeStruct((16, 16, D), BF16),
            jax.ShapeDtypeStruct((16, 16, 128), F32),
        ],
        in_specs=[smem_spec()] * 2 + [vmem_spec()] * 2 + [any_spec()] * 5,
        out_specs=[vmem_spec()] * 2,
        scratch_shapes=[
            pltpu.VMEM((8, 2 * SEQ, D), BF16),
            pltpu.VMEM((2 * SEQ, D), BF16),
            pltpu.VMEM((D, FFL), BF16),
            pltpu.VMEM((D, FFL), BF16),
            pltpu.VMEM((FFP, D), BF16),
            pltpu.VMEM((D, 256), BF16),
            pltpu.VMEM((2 * SEQ, FFP), BF16),
            pairs(8, 16),
            pairs(2, N1A),
            pairs(2, N1 - N1A),
            pairs(2, N1),
            pairs(2, N1),
            pairs(N1),
            pairs(4, 16 - N1),
            pairs(N2A - N1),
            pairs(16 - N2A),
            pairs(16 - N1),
            pairs(16 - N1),
            pairs(16),
            pairs(16),
            pltpu.VMEM((16, D), F32),
            pltpu.VMEM((16, 128), F32),
            pltpu.VMEM((8, 16, 128), F32),
            pltpu.VMEM((16, 128), F32),
            pltpu.VMEM((16, 16, 128), F32),
            pltpu.SemaphoreType.DMA((5,)),
            pltpu.SemaphoreType.DMA((80,)),
            pltpu.SemaphoreType.DMA((80,)),
        ],
        compiler_params=pltpu.CompilerParams(
            collective_id=1, has_side_effects=True, vmem_limit_bytes=60 * 2**20
        ),
    )(
        lengths, destination, row(final_gain), row(score_weight), normed, after, w_gate, w_up,
        w_down,
    )
    hidden_out = jnp.transpose(relaid, (1, 0, 2))

    group_index = lax.axis_index(DP)
    pair_score = scores[:, :, 0].reshape(-1)
    query_total = lax.axis_size(DP) * QUERY_DP
    membership = query_of[:, None] == jnp.arange(query_total, dtype=jnp.int32)[None, :]
    means = jnp.sum(jnp.where(membership, pair_score[:, None], 0.0), axis=0) / (
        pair_score.shape[0] // query_total
    )
    own_mean = jnp.sum(jnp.where(membership, means[None, :], 0.0), axis=1)
    here = (destination == group_index).reshape(16, 16)
    centred = jnp.sum(jnp.where(here, (pair_score - own_mean).reshape(16, 16), 0.0), axis=1)
    query_mean = lax.dynamic_slice_in_dim(means, group_index * QUERY_DP, QUERY_DP)
    return (hidden_out, centred, query_mean)


def solution(mesh):
    split = Mesh(mesh.devices.reshape(4, 2, 2, 4, 2), AXES)
    placed = (
        P(DP + TENSOR, None, None),
        P(),
        P(),
        P(),
        P(),
        P(None, TENSOR),
        P(TENSOR),
        P(),
        P(),
        P(),
        P(TENSOR, None),
        P(),
        P(None, TENSOR),
        P(None, TENSOR),
        P(TENSOR, None),
        P(),
        P(),
    )
    return jax.shard_map(
        on_device,
        mesh=split,
        in_specs=placed,
        out_specs=(P(TENSOR, DP, None), P(DP), P(DP)),
        check_vma=False,
    )
```

time: 445 us -> 186 us (0.42)
  waiting for transfers between devices: 275 us -> 0 us
  Pallas kernels: 0 us -> 164 us
  blocking collectives: 57.6 us -> 0 us
  matrix products: 42 us -> 0 us
  starting transfers between devices: 17.3 us -> 0 us
  between operations: 14.1 us -> 0.68 us
  other arithmetic: 14 us -> 0.85 us
    all_gather x3 -> x0, waiting for transfers between devices: 169 us -> none  [the longest x1 88.1 us: on_device(): piece_rows = lax.all_gather(normed_mlp, TENSOR, axis=0, tiled=True)]
    pallas_call x0 -> x2, Pallas kernels: none -> 164 us  [the longest x1 120 us: on_device(): pl.pallas_call(mlp_kernel, out_shape=[jax.ShapeDtypeStruct((16, 16, D), B...]
    reduce_scatter x1 -> x0, waiting for transfers between devices: 95.8 us -> none  [on_device(): lax.psum_scatter(jnp.einsum('spf,fd->spd', activated, w_down, preferred_e...]
    all_to_all x3 -> x0, blocking collectives: 43.7 us -> none  [the longest x1 19.4 us: on_device(): lax.all_to_all(sorted_rows, 'dp', split_axis=1, concat_axis=1, tiled=True)]
    dot_general x10 -> x0, matrix products: 42 us -> none  [the longest x1 10.6 us: on_device(): jnp.einsum('spd,df->spf', piece_rows, w_up, preferred_element_type=jnp.fl...]
    all_to_all x2 -> x0, starting transfers between devices: 17 us -> none  [the longest x1 8.69 us: copy_for_each(): return lax.all_to_all(copies, axis, split_axis=0, concat_axis=0, tiled=True)]
    all_gather x1 -> x0, blocking collectives: 13.9 us -> none  [gather_axes(): x = lax.all_gather(x, axis, axis=dim, tiled=True)]
    all_to_all x2 -> x0, waiting for transfers between devices: 10.4 us -> none  [the longest x1 7.33 us: on_device(): lax.all_to_all(arrived, TENSOR, split_axis=1, concat_axis=0, tiled=True)]
  transfers between devices with their start and end apart: 6 -> 0, of which waited for: 6 -> 0; matrix products, arithmetic and copies ran while one was open for 6% -> 0% of each run, Pallas kernels for 0% -> 0%
where the time goes in v1:
time: 186 us
  Pallas kernels  164 us (88%)
  local copies, waits for them, and re-layouts  20.3 us (11%)
    pallas_call x1, Pallas kernels, on_device(): pl.pallas_call(mlp_kernel, out_shape=[jax.ShapeDtypeStruct((16, 16, D), B...  120 us
    pallas_call x1, Pallas kernels, on_device(): pl.pallas_call(attention_kernel, out_shape=[jax.ShapeDtypeStruct((2 * SEQ...  43.5 us
    unnamed x9, local copies, waits for them, and re-layouts  12.1 us
    reshape x5, local copies, waits for them, and re-layouts, on_device(): row = lambda v: v.reshape(1, -1)  6.35 us

profile of v1, /device:TPU:1, one launch (start us, length us, event | category | flops | bytes accessed | tf_op | source)
XLA Modules:
  0.0 185.7 jit_solution(7999215909778083010)
XLA Ops:
  0.6 1.3 reshape.35.final_gain
  1.9 1.3 reshape.36.score_weight
  3.2 1.3 reshape.37.gain
  4.5 1.3 reshape.38.mlp_gain
  5.8 1.2 reshape.40.v_bias
  7.0 43.5 %shard_map.202 = (bf16[256,1536]{1,0:T(8,128)(2,1)}, bf16[256,1536]{1,0:T(8,128)(2,1)}) custom-call(s32[256]{0:T(256)} %lengths.3, f32[1,1536]{1,0:T(1,128)} %reshape.37.gain, f32[1,1536]{1,0:T(1,128)} %reshape.38.mlp_gain, bf16[1,128]{1,0:T(2,128)(2,1)} %bitcast.3, bf16[1,256]{1,0:T(2,128)(2,1)} %reshape.40.v_bias, f32[128,128]{1,0:T(8,128)} %constant.32.clone.cosine, ...), custom_call_target="tpu_custom_call" | custom-call | tf_op jit(solution)/shard_map/pallas_call | solution.py:545
  50.5 0.0 copy-start
  50.5 5.8 %copy.28.w_gate = bf16[1536,1120]{1,0:T(8,128)(2,1)} copy(bf16[1536,1120]{0,1:T(8,128)(2,1)} %param.31) | data formatting | bytes 6881280 | tf_op args[12]
  56.3 0.0 copy-done
  56.3 3.8 %copy.29.w_up = bf16[1536,1120]{1,0:T(8,128)(2,1)} copy(bf16[1536,1120]{0,1:T(8,128)(2,1)S(1)} %copy-done) | data formatting | bytes 6881280 | tf_op args[13]
  60.2 0.0 copy-start.2
  60.2 0.0 copy-start.1
  60.2 120.4 %shard_map.203 = (bf16[16,16,1536]{2,1,0:T(8,128)(2,1)}, f32[16,16,128]{2,1,0:T(8,128)}) custom-call(s32[256]{0:T(256)} %lengths.3, s32[256]{0:T(256)} %destination.1, f32[1,1536]{1,0:T(1,128)} %reshape.35.final_gain, f32[1,1536]{1,0:T(1,128)} %reshape.36.score_weight, bf16[256,1536]{1,0:T(8,128)(2,1)} %get-tuple-element.7.normed, ...), custom_call_target="tpu_custom_call" | custom-call | tf_op jit(solution)/shard_map/pallas_call | solution.py:575
  180.6 2.4 %copy.30 = bf16[16,16,1536]{2,1,0:T(8,128)(2,1)} copy(bf16[16,16,1536]{2,0,1:T(8,128)(2,1)} %bitcast.2) | data formatting | bytes 1572864
  183.0 0.0 copy-done.2
  183.0 0.1 reshape.41
  183.1 1.0 slice_reduce_fusion
  184.1 0.1 broadcast_in_dim.31
  184.2 0.0 copy-done.1
  184.2 0.1 select_reduce_fusion.1
  184.3 0.1 select_reduce_fusion
  184.4 0.1 reduce_sum.31
  184.5 0.6 select_reduce_fusion.2
  185.2 0.6 dynamic_slice.3
  (2 shorter events, 0.0 us)
Async XLA Ops:
  50.5 5.8 %copy-start = (bf16[1536,1120]{0,1:T(8,128)(2,1)S(1)}, bf16[1536,1120]{0,1:T(8,128)(2,1)}, u32[]{:S(2)}) copy-start(bf16[1536,1120]{0,1:T(8,128)(2,1)} %param.32) | copy-start | bytes 10321924
  60.2 122.8 %copy-start.2 = (s32[256]{0:T(256)S(1)}, s32[256]{0:T(256)}, u32[]{:S(2)}) copy-start(s32[256]{0:T(256)} %destination.1) | copy-start | bytes 3076
  60.2 124.0 %copy-start.1 = (s32[256]{0:T(256)S(1)}, s32[256]{0:T(256)}, u32[]{:S(2)}) copy-start(s32[256]{0:T(256)} %param.21) | copy-start | bytes 3076

commit v2 on v1

v2 whole, which is shorter than its diff:
```python
import functools
import math

import jax
import jax.numpy as jnp
import numpy as np
from jax import lax
from jax.experimental import pallas as pl
from jax.experimental.pallas import tpu as pltpu
from jax.sharding import Mesh
from jax.sharding import PartitionSpec as P

AXES = ("y", "xl", "c", "z", "xh")
DP = ("y", "xl", "c")
TENSOR = ("z", "xh")
MESH = pl.DeviceIdType.MESH
F32 = jnp.float32
BF16 = jnp.bfloat16

KV_HEADS = 2
HEAD_DIM = 128
HEADS = 8
QUERY_DP = 2
theta_base = 1000000.0
norm_eps = 1e-06

SEQ = 128
D = 1536
FFL = 1120
FULL = 1024
TAIL = FFL - FULL
FFP = 1152

C1 = (0, 144)
C1A, C1B = (0, 80), (80, 144)
C2 = (144, 256)
C2A, C2B = (144, 208), (208, 256)
N1, N1A = 9, 5
N2A = 13


def z_at(step):
    return lax.rem(lax.axis_index("z") + step + 4, 4)


class Sender:
    def __init__(self, send_sem, recv_sem):
        self.send_sem, self.recv_sem, self.count = send_sem, recv_sem, 0
        self.open = []

    def __call__(self, src, dst, device):
        i = self.count
        self.count += 1
        copy = pltpu.make_async_remote_copy(
            src_ref=src,
            dst_ref=dst,
            send_sem=self.send_sem.at[i],
            recv_sem=self.recv_sem.at[i],
            device_id=device,
            device_id_type=MESH,
        )
        copy.start()
        self.open.append(copy)
        return copy

    def drain(self):
        for copy in self.open:
            copy.wait_send()
        self.open = []


def tensor_peer(k):
    index = lax.rem(lax.axis_index("z") * 2 + lax.axis_index("xh") + k, 8)
    return {"z": index // 2, "xh": lax.rem(index, 2)}


def dp_peer(k):
    index = lax.axis_index("y") * 4 + lax.axis_index("xl") * 2 + lax.axis_index("c")
    index = lax.rem(index + k, 16)
    return index, {"y": index // 4, "xl": lax.rem(index // 2, 2), "c": lax.rem(index, 2)}


def greet(devices):
    barrier = pltpu.get_barrier_semaphore()
    for device in devices:
        pl.semaphore_signal(barrier, inc=1, device_id=device, device_id_type=MESH)
    pl.semaphore_wait(barrier, len(devices))


def rms_rows(values, gain):
    scale = lax.rsqrt(jnp.mean(values * values, axis=-1, keepdims=True) + norm_eps)
    return values * scale * gain


def rotate(values, cosine, sine):
    return values * cosine + pltpu.roll(values, HEAD_DIM // 2, 1) * sine


def layer_kernel(
    lengths, destination, gain, mlp_gain, final_gain, score_weight, q_bias, v_bias, cosine, sine,
    arrived, q_w, k_w, v_w, o_w, w_gate, w_up, w_down,
    relaid_out, scores_out,
    x_v, k_v, v_v, q_all, o_all, bias_one, bias_all, normed, keys, values, queries, context,
    after_v, gathered, wg, wu, wd, w_tail, active, partial,
    r1_low, r1_high, r1_up, r1_down, r1_x, r2_x, r2_low, r2_high, r2_up, r2_down,
    staged, landed, squares, dots, score_one, score_eight, score_sum, score_all,
    local_sem, send_sem, recv_sem,
):
    z, xh, c = lax.axis_index("z"), lax.axis_index("xh"), lax.axis_index("c")
    y, xl = lax.axis_index("y"), lax.axis_index("xl")
    t = z * 2 + xh
    b = y * 4 + xl * 2 + c
    partner, sibling = {"xh": 1 - xh}, {"c": 1 - c}
    up, down = {"z": z_at(1)}, {"z": z_at(-1)}
    zp, zm, z2 = z_at(1), z_at(-1), z_at(2)
    here, there = t, z * 2 + 1 - xh
    low, high = zm * 2 + xh, zp * 2 + xh
    low_x, high_x = zm * 2 + 1 - xh, zp * 2 + 1 - xh
    far, far_x = z2 * 2 + xh, z2 * 2 + 1 - xh

    def q_cols(index):
        return pl.ds(pl.multiple_of(index * HEAD_DIM, HEAD_DIM), HEAD_DIM)

    sources = [
        (arrived, x_v),
        (k_w, k_v),
        (v_w, v_v),
        (q_w, q_all.at[:, q_cols(t)]),
        (o_w, o_all.at[pl.ds(pl.multiple_of(t * HEAD_DIM, HEAD_DIM), HEAD_DIM)]),
        (w_gate, wg),
        (w_up, wu),
        (w_down, wd.at[pl.ds(0, FFL)]),
        (w_gate.at[pl.ds(FULL, TAIL)], w_tail.at[pl.ds(0, TAIL)]),
        (w_up.at[pl.ds(FULL, TAIL)], w_tail.at[pl.ds(128, TAIL)]),
    ]
    loads = [
        pltpu.make_async_copy(src, dst, local_sem.at[i]) for i, (src, dst) in enumerate(sources)
    ]
    for load in loads[:5]:
        load.start()
    bias_one[...] = jnp.broadcast_to(q_bias[...].reshape(1, HEAD_DIM).astype(F32), bias_one.shape)
    greet([tensor_peer(k) for k in range(1, 8)] + [dp_peer(k)[1] for k in range(1, 16)])
    send = Sender(send_sem, recv_sem)

    half_q, half_o = D // 2, HEAD_DIM // 2

    def q_piece(index, sub=None):
        size = half_q if sub is None else half_q // 2
        start = c * half_q + (0 if sub is None else sub * size)
        return q_all.at[pl.ds(pl.multiple_of(start, 128), size), q_cols(index)]

    def o_piece(index, sub=None):
        size = half_o if sub is None else half_o // 2
        start = index * HEAD_DIM + c * half_o + (0 if sub is None else sub * size)
        return o_all.at[pl.ds(pl.multiple_of(start, 32), size)]

    own_q = q_w.at[pl.ds(pl.multiple_of(c * half_q, 128), half_q)]
    own_o = o_w.at[pl.ds(pl.multiple_of(c * half_o, 64), half_o)]

    o_u, o_d = send(own_o, o_piece(t), up), send(own_o, o_piece(t), down)
    q_x = send(own_q, q_piece(t), partner)
    q_u, q_d = send(own_q, q_piece(t), up), send(own_q, q_piece(t), down)
    bias_copies = [send(bias_one, bias_all.at[t], tensor_peer(k)) for k in range(1, 8)]
    o_x = send(own_o, o_piece(t), partner)
    for load in loads[5:]:
        load.start()

    loads[0].wait()
    x = x_v[...].reshape(2 * SEQ, D)
    normed[...] = rms_rows(x.astype(F32), gain[...].reshape(1, D)).astype(BF16)
    loads[1].wait()
    loads[2].wait()
    cos_rows = jnp.concatenate([cosine[...]] * 2, axis=0)
    sin_rows = jnp.concatenate([sine[...]] * 2, axis=0)
    k_f = jnp.dot(normed[...], k_v[...], preferred_element_type=F32)
    for g in range(KV_HEADS):
        cols = slice(g * HEAD_DIM, (g + 1) * HEAD_DIM)
        keys[:, cols] = rotate(k_f[:, cols], cos_rows, sin_rows).astype(BF16)
    v_f = jnp.dot(normed[...], v_v[...], preferred_element_type=F32)
    values[...] = (v_f + v_bias[...].reshape(1, -1).astype(F32)).astype(BF16)

    q_sib, o_sib = [], []

    def share(piece, index, sub, copies):
        copies.append(send(piece(index, sub), piece(index, sub), sibling))

    def pass_piece(piece, index, sub, device):
        return send(piece(index, sub), piece(index, sub), device)

    o_u.wait_recv()
    o_fu = pass_piece(o_piece, low, 0, up)
    o_xl = pass_piece(o_piece, low, None, partner)
    share(o_piece, low, None, o_sib)
    o_d.wait_recv()
    o_fd = pass_piece(o_piece, high, 1, down)
    o_xh = pass_piece(o_piece, high, None, partner)
    share(o_piece, high, None, o_sib)
    q_x.wait_recv()
    q_xu = pass_piece(q_piece, there, None, up)
    q_xd = pass_piece(q_piece, there, None, down)
    share(q_piece, there, None, q_sib)
    q_u.wait_recv()
    q_fu = pass_piece(q_piece, low, 0, up)
    share(q_piece, low, None, q_sib)
    q_d.wait_recv()
    q_fd = pass_piece(q_piece, high, 1, down)
    share(q_piece, high, None, q_sib)
    o_fu.wait_recv()
    o_xfa = pass_piece(o_piece, far, 0, partner)
    share(o_piece, far, 0, o_sib)
    o_fd.wait_recv()
    o_xfb = pass_piece(o_piece, far, 1, partner)
    share(o_piece, far, 1, o_sib)
    o_x.wait_recv()
    share(o_piece, there, None, o_sib)
    q_xu.wait_recv()
    q_fxu = pass_piece(q_piece, low_x, 0, up)
    share(q_piece, low_x, None, q_sib)
    q_xd.wait_recv()
    q_fxd = pass_piece(q_piece, high_x, 1, down)
    share(q_piece, high_x, None, q_sib)
    o_xl.wait_recv()
    share(o_piece, low_x, None, o_sib)
    q_fu.wait_recv()
    share(q_piece, far, 0, q_sib)
    q_fd.wait_recv()
    share(q_piece, far, 1, q_sib)
    o_xh.wait_recv()
    share(o_piece, high_x, None, o_sib)
    q_fxu.wait_recv()
    share(q_piece, far_x, 0, q_sib)
    q_fxd.wait_recv()
    share(q_piece, far_x, 1, q_sib)
    for copy in q_sib:
        copy.wait_recv()
    loads[3].wait()
    for copy in bias_copies:
        copy.wait_recv()
    bias_all[t] = bias_one[...]

    def project_q(i, carry):
        cols = pl.ds(pl.multiple_of(i * 256, 256), 256)
        q_f = jnp.dot(normed[...], q_all[:, cols], preferred_element_type=F32)
        for e in range(2):
            q_e = q_f[:, e * HEAD_DIM : (e + 1) * HEAD_DIM] + bias_all[2 * i + e][0:1]
            at = pl.ds(pl.multiple_of(i * 256 + e * HEAD_DIM, HEAD_DIM), HEAD_DIM)
            queries[:, at] = rotate(q_e, cos_rows, sin_rows).astype(BF16)
        return carry

    lax.fori_loop(0, HEADS // 2, project_q, 0)

    o_xfa.wait_recv()
    share(o_piece, far_x, 0, o_sib)
    o_xfb.wait_recv()
    share(o_piece, far_x, 1, o_sib)

    q_pos = lax.broadcasted_iota(jnp.int32, (SEQ, SEQ), 0)
    k_pos = lax.broadcasted_iota(jnp.int32, (SEQ, SEQ), 1)
    group = HEADS // KV_HEADS
    first_pair = (b * 8 + t) * 2
    for p in range(2):
        rows = slice(p * SEQ, (p + 1) * SEQ)
        allowed = (k_pos <= q_pos) & (k_pos < lengths[first_pair + p])
        allowed = jnp.concatenate([allowed.astype(F32)] * group, axis=0) > 0.5
        for g in range(KV_HEADS):
            cols = slice(g * HEAD_DIM, (g + 1) * HEAD_DIM)
            q_g = jnp.concatenate(
                [
                    queries[rows, (g * group + h) * HEAD_DIM : (g * group + h + 1) * HEAD_DIM]
                    for h in range(group)
                ],
                axis=0,
            )
            logits = lax.dot_general(
                q_g, keys[rows, cols], (((1,), (1,)), ((), ())), preferred_element_type=F32
            ) / math.sqrt(HEAD_DIM)
            logits = jnp.where(allowed, logits, -1e30)
            shifted = jnp.exp(logits - jnp.max(logits, axis=-1, keepdims=True))
            probs = (shifted / jnp.sum(shifted, axis=-1, keepdims=True)).astype(BF16)
            ctx = jnp.dot(probs, values[rows, cols], preferred_element_type=F32).astype(BF16)
            for h in range(group):
                at = (g * group + h) * HEAD_DIM
                context[rows, at : at + HEAD_DIM] = ctx[h * SEQ : (h + 1) * SEQ]

    for copy in o_sib:
        copy.wait_recv()
    loads[4].wait()

    def project_out(i, carry):
        cols = pl.ds(pl.multiple_of(i * 256, 256), 256)
        attended = jnp.dot(context[...], o_all[:, cols], preferred_element_type=F32)
        base = x_v[:, :, cols].reshape(2 * SEQ, 256).astype(F32)
        after_v[:, cols] = (base + attended).astype(BF16)
        return carry

    lax.fori_loop(0, D // 256, project_out, 0)
    gathered[t] = rms_rows(after_v[...].astype(F32), mlp_gain[...].reshape(1, D)).astype(BF16)

    def block_rows(g, span):
        return gathered.at[g, pl.ds(span[0], span[1] - span[0])]

    def pass_on(g, span, device):
        return send(block_rows(g, span), block_rows(g, span), device)

    u2 = pass_on(here, C2, up)
    d2 = pass_on(here, C2, down)
    x1 = pass_on(here, C1, partner)
    u1 = pass_on(here, C1, up)
    d1 = pass_on(here, C1, down)
    x2 = pass_on(here, C2, partner)

    for load in loads[5:]:
        load.wait()
    wd[FFL:FFP] = jnp.zeros((FFP - FFL, D), BF16)
    w_tail[TAIL:128] = jnp.zeros((128 - TAIL, D), BF16)
    w_tail[128 + TAIL :] = jnp.zeros((128 - TAIL, D), BF16)

    def gated(gate_values, up_values):
        return (gate_values / (1.0 + jnp.exp(-gate_values)) * up_values).astype(BF16)

    def by_rows(g, weights):
        return lax.dot_general(
            gathered[g], weights, (((1,), (1,)), ((), ())), preferred_element_type=F32
        )

    def block(g, own=False):
        def hidden(i, carry):
            at = pl.ds(pl.multiple_of(i * 256, 256), 256)
            active[:, at] = gated(by_rows(g, wg[at]), by_rows(g, wu[at]))
            return carry

        lax.fori_loop(0, FULL // 256, hidden, 0)
        both = by_rows(g, w_tail[...])
        active[:, FULL:FFP] = gated(both[:, :128], both[:, 128:])

        def project(i, carry):
            cols = pl.ds(pl.multiple_of(i * 256, 256), 256)
            result = jnp.dot(active[...], wd[:, cols], preferred_element_type=F32)
            if own:
                result = result.astype(BF16).astype(F32) + after_v[:, cols].astype(F32)
            result = result.astype(BF16).reshape(2, 8, 16, 256)
            for owner in range(8):
                partial[owner, pl.ds(2 * g, 2), :, cols] = result[:, owner]
            return carry

        lax.fori_loop(0, D // 256, project, 0)

    block(here, own=True)
    u2.wait_recv()
    f2u = pass_on(low, C2A, up)
    x_low = pass_on(low, C2, partner)
    d2.wait_recv()
    f2d = pass_on(high, C2B, down)
    x_high = pass_on(high, C2, partner)
    x1.wait_recv()
    xu = pass_on(there, C1, up)
    xd = pass_on(there, C1, down)
    u1.wait_recv()
    f1u = pass_on(low, C1A, up)
    d1.wait_recv()
    f1d = pass_on(high, C1B, down)
    block(low)
    f2u.wait_recv()
    x_far_a = pass_on(far, C2A, partner)
    f2d.wait_recv()
    x_far_b = pass_on(far, C2B, partner)
    block(high)
    x2.wait_recv()
    block(there)
    xu.wait_recv()
    fxu = pass_on(low_x, C1A, up)
    xd.wait_recv()
    fxd = pass_on(high_x, C1B, down)
    x_low.wait_recv()
    block(low_x)
    x_high.wait_recv()
    block(high_x)
    f1u.wait_recv()
    f1d.wait_recv()
    block(far)
    fxu.wait_recv()
    fxd.wait_recv()
    x_far_a.wait_recv()
    x_far_b.wait_recv()
    block(far_x)

    def add_both(cols, zz, lo, extra):
        def step(i, carry):
            for e in range(2):
                at = (2 * zz + e, lo + i, slice(None), cols)
                partial[at] = (
                    partial[at].astype(F32) + extra[e, i, :, cols].astype(F32)
                ).astype(BF16)
            return carry

        lax.fori_loop(0, extra.shape[1], step, 0)

    def add_one(cols, index, lo, extra):
        def step(i, carry):
            at = (index, lo + i, slice(None), cols)
            partial[at] = (partial[at].astype(F32) + extra[i, :, cols].astype(F32)).astype(BF16)
            return carry

        lax.fori_loop(0, extra.shape[0], step, 0)

    class Half:
        def __init__(self, h):
            self.h = h
            self.cols = slice(h * (D // 2), (h + 1) * (D // 2))

        def both_of(self, zz, lo, hi):
            return partial.at[pl.ds(2 * zz, 2), pl.ds(lo, hi - lo), :, self.cols]

        def one_of(self, index, lo, hi):
            return partial.at[index, pl.ds(lo, hi - lo), :, self.cols]

        def begin(self):
            cols = self.cols
            self.a_up = send(self.both_of(z2, 0, N1A), r1_low.at[:, :, :, cols], up)
            self.a_down = send(self.both_of(z2, N1A, N1), r1_high.at[:, :, :, cols], down)

        def cross(self, k):
            zz = (z2, zp, zm, z)[k]
            return send(
                self.one_of(zz * 2 + 1 - xh, N1, 16), r2_x.at[k, :, :, self.cols], partner
            )

        def middle(self):
            cols = self.cols
            self.a_up.wait_recv()
            add_both(cols, zp, 0, r1_low)
            self.b_up = send(self.both_of(zp, 0, N1), r1_up.at[:, :, :, cols], up)
            self.a_down.wait_recv()
            add_both(cols, zm, N1A, r1_high)
            self.b_down = send(self.both_of(zm, 0, N1), r1_down.at[:, :, :, cols], down)

        def second(self, sx):
            cols = self.cols
            sx[0].wait_recv()
            add_one(cols, far, N1, r2_x.at[0])
            self.c_up = send(self.one_of(far, N1, N2A), r2_low.at[:, :, cols], up)
            self.c_down = send(self.one_of(far, N2A, 16), r2_high.at[:, :, cols], down)
            sx[1].wait_recv()
            add_one(cols, high, N1, r2_x.at[1])
            sx[2].wait_recv()
            add_one(cols, low, N1, r2_x.at[2])

        def third(self):
            cols = self.cols
            self.c_up.wait_recv()
            add_one(cols, high, N1, r2_low)
            self.e_up = send(self.one_of(high, N1, 16), r2_up.at[:, :, cols], up)
            self.c_down.wait_recv()
            add_one(cols, low, N2A, r2_high)
            self.e_down = send(self.one_of(low, N1, 16), r2_down.at[:, :, cols], down)

        def fold(self):
            cols = self.cols
            self.b_up.wait_recv()
            self.b_down.wait_recv()

            def step(i, carry):
                at = (there, i, slice(None), cols)
                total = partial[at].astype(F32) + r1_up[1 - xh, i, :, cols].astype(F32)
                partial[at] = (total + r1_down[1 - xh, i, :, cols].astype(F32)).astype(BF16)
                return carry

            lax.fori_loop(0, N1, step, 0)
            self.ex = send(self.one_of(there, 0, N1), r1_x.at[:, :, cols], partner)

        def finish(self, sx):
            cols = self.cols
            sx[3].wait_recv()
            add_one(cols, t, N1, r2_x.at[3])
            self.e_up.wait_recv()
            self.e_down.wait_recv()

            def two(i, carry):
                at = (t, N1 + i, slice(None), cols)
                total = partial[at].astype(F32) + r2_up[i, :, cols].astype(F32)
                partial[at] = (total + r2_down[i, :, cols].astype(F32)).astype(BF16)
                return carry

            lax.fori_loop(0, 16 - N1, two, 0)
            self.ex.wait_recv()

            def one(i, carry):
                at = (t, i, slice(None), cols)
                total = partial[at].astype(F32) + r1_up[xh, i, :, cols].astype(F32)
                total = total + r1_down[xh, i, :, cols].astype(F32)
                partial[at] = (total + r1_x[i, :, cols].astype(F32)).astype(BF16)
                return carry

            lax.fori_loop(0, N1, one, 0)

        def relay(self):
            cols = self.cols
            copies = []
            for k in range(16):
                device = dp_peer(k)[1]
                if k == 0:
                    landed[b, :, cols] = partial[t, chosen[k], :, cols]
                else:
                    staged[k, :, cols] = partial[t, chosen[k], :, cols]
                    copies.append(
                        send(staged.at[k, :, cols], landed.at[b, :, cols], device)
                    )
            return copies

        def score(self):
            cols = self.cols
            weight = (final_gain[...] * score_weight[...]).reshape(1, D)[:, cols]
            position = lax.broadcasted_iota(jnp.int32, (16, D // 2), 0)
            for p in range(16):
                wanted = lengths[b * 16 + p] - 1 - t * 16
                row = jnp.where(position == wanted, partial[t, p, :, cols].astype(F32), 0.0)
                row = jnp.sum(row, axis=0, keepdims=True)
                sums = jnp.sum(row * row, axis=-1, keepdims=True)
                squares[self.h, p : p + 1] = jnp.broadcast_to(sums, (1, 128))
                sums = jnp.sum(row * weight, axis=-1, keepdims=True)
                dots[self.h, p : p + 1] = jnp.broadcast_to(sums, (1, 128))

    chosen = []
    for k in range(16):
        index = dp_peer(k)[0]
        pair = jnp.int32(0)
        for j in range(1, 16):
            pair = jnp.where(destination[b * 16 + j] == index, j, pair)
        chosen.append(pair)

    h0, h1 = Half(0), Half(1)
    h0.begin()
    sx0 = [h0.cross(k) for k in range(4)]
    h1.begin()
    sx1 = [h1.cross(0)]
    h0.middle()
    h0.second(sx0)
    h0.third()
    h0.fold()
    sx1 += [h1.cross(k) for k in range(1, 4)]
    h1.middle()
    h0.finish(sx0)
    pair_copies = h0.relay()
    h0.score()
    h1.second(sx1)
    h1.third()
    h1.fold()
    h1.finish(sx1)
    pair_copies += h1.relay()
    h1.score()

    mean = (squares[0] + squares[1]) / D
    score_one[...] = (dots[0] + dots[1]) * lax.rsqrt(mean + norm_eps)
    copies = [send(score_one, score_eight.at[t], tensor_peer(k)) for k in range(1, 8)]
    score_eight[t] = score_one[...]
    for copy in copies:
        copy.wait_recv()
    total = score_eight[0]
    for k in range(1, 8):
        total = total + score_eight[k]
    score_sum[...] = total
    score_all[b] = total
    copies = [send(score_sum, score_all.at[b], dp_peer(k)[1]) for k in range(1, 16)]
    for copy in copies:
        copy.wait_recv()
    scores_out[...] = score_all[...]
    for copy in pair_copies:
        copy.wait_recv()
    relaid_out[...] = landed[...]
    send.drain()


def any_spec():
    return pl.BlockSpec(memory_space=pl.ANY)


def vmem_spec():
    return pl.BlockSpec(memory_space=pltpu.VMEM)


def smem_spec():
    return pl.BlockSpec(memory_space=pltpu.SMEM)


def rotary_tables():
    index = np.arange(HEAD_DIM // 2, dtype=np.float32)
    frequency = np.power(np.float64(theta_base), -2.0 * index / HEAD_DIM).astype(np.float32)
    angles = np.arange(SEQ, dtype=np.float32)[:, None] * frequency[None, :]
    cosine, sine = np.cos(angles.astype(np.float64)), np.sin(angles.astype(np.float64))
    return (
        np.concatenate([cosine, cosine], axis=1).astype(np.float32),
        np.concatenate([-sine, sine], axis=1).astype(np.float32),
    )


def on_device(
    arrived, destination, query_of, lengths, attn_gain, q_weight, q_bias, k_weight, v_weight,
    v_bias, o_weight, mlp_gain, w_gate, w_up, w_down, final_gain, score_weight,
):
    cosine, sine = rotary_tables()
    pairs = lambda *lead: pltpu.VMEM((*lead, 16, D), BF16)
    relaid, scores = pl.pallas_call(
        layer_kernel,
        out_shape=[
            jax.ShapeDtypeStruct((16, 16, D), BF16),
            jax.ShapeDtypeStruct((16, 16, 128), F32),
        ],
        in_specs=[smem_spec()] * 2 + [vmem_spec()] * 8 + [any_spec()] * 8,
        out_specs=[vmem_spec()] * 2,
        scratch_shapes=[
            pltpu.VMEM((2, SEQ, D), BF16),
            pltpu.VMEM((D, KV_HEADS * HEAD_DIM), BF16),
            pltpu.VMEM((D, KV_HEADS * HEAD_DIM), BF16),
            pltpu.VMEM((D, HEADS * HEAD_DIM), BF16),
            pltpu.VMEM((HEADS * HEAD_DIM, D), BF16),
            pltpu.VMEM((8, HEAD_DIM), F32),
            pltpu.VMEM((8, 8, HEAD_DIM), F32),
            pltpu.VMEM((2 * SEQ, D), BF16),
            pltpu.VMEM((2 * SEQ, KV_HEADS * HEAD_DIM), BF16),
            pltpu.VMEM((2 * SEQ, KV_HEADS * HEAD_DIM), BF16),
            pltpu.VMEM((2 * SEQ, HEADS * HEAD_DIM), BF16),
            pltpu.VMEM((2 * SEQ, HEADS * HEAD_DIM), BF16),
            pltpu.VMEM((2 * SEQ, D), BF16),
            pltpu.VMEM((8, 2 * SEQ, D), BF16),
            pltpu.VMEM((FFL, D), BF16),
            pltpu.VMEM((FFL, D), BF16),
            pltpu.VMEM((FFP, D), BF16),
            pltpu.VMEM((256, D), BF16),
            pltpu.VMEM((2 * SEQ, FFP), BF16),
            pairs(8, 16),
            pairs(2, N1A),
            pairs(2, N1 - N1A),
            pairs(2, N1),
            pairs(2, N1),
            pairs(N1),
            pairs(4, 16 - N1),
            pairs(N2A - N1),
            pairs(16 - N2A),
            pairs(16 - N1),
            pairs(16 - N1),
            pairs(16),
            pairs(16),
            pltpu.VMEM((2, 16, 128), F32),
            pltpu.VMEM((2, 16, 128), F32),
            pltpu.VMEM((16, 128), F32),
            pltpu.VMEM((8, 16, 128), F32),
            pltpu.VMEM((16, 128), F32),
            pltpu.VMEM((16, 16, 128), F32),
            pltpu.SemaphoreType.DMA((10,)),
            pltpu.SemaphoreType.DMA((144,)),
            pltpu.SemaphoreType.DMA((144,)),
        ],
        compiler_params=pltpu.CompilerParams(
            collective_id=0, has_side_effects=True, vmem_limit_bytes=60 * 2**20
        ),
    )(
        lengths, destination, attn_gain, mlp_gain, final_gain, score_weight, q_bias, v_bias,
        cosine, sine, arrived, q_weight, k_weight, v_weight, o_weight, w_gate.T, w_up.T, w_down,
    )
    hidden_out = jnp.transpose(relaid, (1, 0, 2))

    group_index = lax.axis_index(DP)
    pair_score = scores[:, :, 0].reshape(-1)
    query_total = lax.axis_size(DP) * QUERY_DP
    membership = query_of[:, None] == jnp.arange(query_total, dtype=jnp.int32)[None, :]
    means = jnp.sum(jnp.where(membership, pair_score[:, None], 0.0), axis=0) / (
        pair_score.shape[0] // query_total
    )
    own_mean = jnp.sum(jnp.where(membership, means[None, :], 0.0), axis=1)
    here = (destination == group_index).reshape(16, 16)
    centred = jnp.sum(jnp.where(here, (pair_score - own_mean).reshape(16, 16), 0.0), axis=1)
    query_mean = lax.dynamic_slice_in_dim(means, group_index * QUERY_DP, QUERY_DP)
    return (hidden_out, centred, query_mean)


def solution(mesh):
    split = Mesh(mesh.devices.reshape(4, 2, 2, 4, 2), AXES)
    placed = (
        P(DP + TENSOR, None, None),
        P(),
        P(),
        P(),
        P(),
        P(None, TENSOR),
        P(TENSOR),
        P(),
        P(),
        P(),
        P(TENSOR, None),
        P(),
        P(None, TENSOR),
        P(None, TENSOR),
        P(TENSOR, None),
        P(),
        P(),
    )
    return jax.shard_map(
        on_device,
        mesh=split,
        in_specs=placed,
        out_specs=(P(TENSOR, DP, None), P(DP), P(DP)),
        check_vma=False,
    )
```

time: 186 us -> 164 us (0.88)
  local copies, waits for them, and re-layouts: 20.3 us -> 4.3 us
  Pallas kernels: 164 us -> 158 us
    unnamed x9 -> x5, local copies, waits for them, and re-layouts: 12.1 us -> 2.45 us
    reshape x5 -> x0, local copies, waits for them, and re-layouts: 6.35 us -> none  [on_device(): row = lambda v: v.reshape(1, -1)]
    pallas_call x2 -> x1, Pallas kernels: 164 us -> 158 us  [on_device(): pl.pallas_call(layer_kernel, out_shape=[jax.ShapeDtypeStruct((16, 16, D),...]
where the time goes in v2:
time: 164 us
  Pallas kernels  158 us (96%)
  local copies, waits for them, and re-layouts  4.3 us (3%)
    pallas_call x1, Pallas kernels, on_device(): pl.pallas_call(layer_kernel, out_shape=[jax.ShapeDtypeStruct((16, 16, D),...  158 us

profile of v2, /device:TPU:1, one launch (start us, length us, event | category | flops | bytes accessed | tf_op | source)
XLA Modules:
  0.0 163.7 jit_solution(10218752341751962835)
XLA Ops:
  0.6 0.0 copy-start.1
  0.7 0.0 copy-start
  0.7 157.9 %shard_map.202 = (bf16[16,16,1536]{2,1,0:T(8,128)(2,1)}, f32[16,16,128]{2,1,0:T(8,128)}) custom-call(s32[256]{0:T(256)} %lengths.1, s32[256]{0:T(256)} %destination.1, f32[1536]{0:T(1024)} %gain.1, f32[1536]{0:T(1024)} %mlp_gain.1, f32[1536]{0:T(1024)} %final_gain.1, f32[1536]{0:T(1024)} %score_weight.1, bf16[128]{0:T(256)(128)(2,1)} %q_bias.1, ...), custom_call_target="tpu_custom_call" | custom-call | tf_op jit(solution)/shard_map/pallas_call | solution.py:602
  158.6 1.0 slice_reduce_fusion
  159.6 0.1 broadcast_in_dim.31
  159.7 0.0 copy-done.1
  159.7 0.1 select_reduce_fusion.1
  159.8 0.6 dynamic_slice.3
  160.4 0.0 copy-done
  160.4 0.1 reshape.17
  160.5 0.1 select_reduce_fusion
  160.6 0.1 reduce_sum.31
  160.7 0.6 select_reduce_fusion.2
  161.3 2.4 %copy.24 = bf16[16,16,1536]{2,1,0:T(8,128)(2,1)} copy(bf16[16,16,1536]{2,0,1:T(8,128)(2,1)} %bitcast.5) | data formatting | bytes 1572864
  (2 shorter events, 0.0 us)
Async XLA Ops:
  0.6 159.0 %copy-start.1 = (s32[256]{0:T(256)S(1)}, s32[256]{0:T(256)}, u32[]{:S(2)}) copy-start(s32[256]{0:T(256)} %param.21) | copy-start | bytes 3076
  0.7 159.7 %copy-start = (s32[256]{0:T(256)S(1)}, s32[256]{0:T(256)}, u32[]{:S(2)}) copy-start(s32[256]{0:T(256)} %destination.1) | copy-start | bytes 3076

commit v3 on v2

--- a/solution.py
+++ b/solution.py
@@ -37,6 +37,15 @@
 C2A, C2B = (144, 208), (208, 256)
 N1, N1A = 9, 5
 N2A = 13
+
+
+ORDER = (
+    ("x2", 0), ("x3", 0), ("b", 0), ("x0", 0), ("x1", 0), ("x2", 1), ("b", 1), ("md", 0),
+    ("mu", 0), ("s0", 0), ("x1", 1), ("md", 1), ("x0", 1), ("mu", 1), ("fo", 0), ("s0", 1),
+    ("s2", 1), ("s1", 0), ("s3", 0), ("tu", 0), ("s2", 0), ("td", 0), ("x3", 1), ("s1", 1),
+    ("td", 1), ("fo", 1), ("tu", 1), ("s3", 1), ("f1", 0), ("f2", 0), ("re", 0), ("sc", 0),
+    ("f1", 1), ("f2", 1), ("re", 1), ("sc", 1),
+)
 
 
 def z_at(step):
@@ -247,7 +256,7 @@
             queries[:, at] = rotate(q_e, cos_rows, sin_rows).astype(BF16)
         return carry
 
-    lax.fori_loop(0, HEADS // 2, project_q, 0)
+    lax.fori_loop(0, HEADS // 2, project_q, 0, unroll=True)
 
     o_xfa.wait_recv()
     share(o_piece, far_x, 0, o_sib)
@@ -293,7 +302,7 @@
         after_v[:, cols] = (base + attended).astype(BF16)
         return carry
 
-    lax.fori_loop(0, D // 256, project_out, 0)
+    lax.fori_loop(0, D // 256, project_out, 0, unroll=True)
     gathered[t] = rms_rows(after_v[...].astype(F32), mlp_gain[...].reshape(1, D)).astype(BF16)
 
     def block_rows(g, span):
@@ -329,7 +338,7 @@
             active[:, at] = gated(by_rows(g, wg[at]), by_rows(g, wu[at]))
             return carry
 
-        lax.fori_loop(0, FULL // 256, hidden, 0)
+        lax.fori_loop(0, FULL // 256, hidden, 0, unroll=True)
         both = by_rows(g, w_tail[...])
         active[:, FULL:FFP] = gated(both[:, :128], both[:, 128:])
 
@@ -343,7 +352,7 @@
                 partial[owner, pl.ds(2 * g, 2), :, cols] = result[:, owner]
             return carry
 
-        lax.fori_loop(0, D // 256, project, 0)
+        lax.fori_loop(0, D // 256, project, 0, unroll=True)
 
     block(here, own=True)
     u2.wait_recv()
@@ -393,7 +402,7 @@
                 ).astype(BF16)
             return carry
 
-        lax.fori_loop(0, extra.shape[1], step, 0)
+        lax.fori_loop(0, extra.shape[1], step, 0, unroll=True)
 
     def add_one(cols, index, lo, extra):
         def step(i, carry):
@@ -401,11 +410,11 @@
             partial[at] = (partial[at].astype(F32) + extra[i, :, cols].astype(F32)).astype(BF16)
             return carry
 
-        lax.fori_loop(0, extra.shape[0], step, 0)
+        lax.fori_loop(0, extra.shape[0], step, 0, unroll=True)
 
     class Half:
         def __init__(self, h):
-            self.h = h
+            self.h, self.sx, self.copies = h, [None] * 4, []
             self.cols = slice(h * (D // 2), (h + 1) * (D // 2))
 
         def both_of(self, zz, lo, hi):
@@ -421,38 +430,37 @@
 
         def cross(self, k):
             zz = (z2, zp, zm, z)[k]
-            return send(
+            self.sx[k] = send(
                 self.one_of(zz * 2 + 1 - xh, N1, 16), r2_x.at[k, :, :, self.cols], partner
             )
 
-        def middle(self):
-            cols = self.cols
+        def mid_up(self):
             self.a_up.wait_recv()
-            add_both(cols, zp, 0, r1_low)
-            self.b_up = send(self.both_of(zp, 0, N1), r1_up.at[:, :, :, cols], up)
+            add_both(self.cols, zp, 0, r1_low)
+            self.b_up = send(self.both_of(zp, 0, N1), r1_up.at[:, :, :, self.cols], up)
+
+        def mid_down(self):
             self.a_down.wait_recv()
-            add_both(cols, zm, N1A, r1_high)
-            self.b_down = send(self.both_of(zm, 0, N1), r1_down.at[:, :, :, cols], down)
-
-        def second(self, sx):
-            cols = self.cols
-            sx[0].wait_recv()
-            add_one(cols, far, N1, r2_x.at[0])
-            self.c_up = send(self.one_of(far, N1, N2A), r2_low.at[:, :, cols], up)
-            self.c_down = send(self.one_of(far, N2A, 16), r2_high.at[:, :, cols], down)
-            sx[1].wait_recv()
-            add_one(cols, high, N1, r2_x.at[1])
-            sx[2].wait_recv()
-            add_one(cols, low, N1, r2_x.at[2])
-
-        def third(self):
-            cols = self.cols
+            add_both(self.cols, zm, N1A, r1_high)
+            self.b_down = send(self.both_of(zm, 0, N1), r1_down.at[:, :, :, self.cols], down)
+
+        def crossed(self, k):
+            self.sx[k].wait_recv()
+            add_one(self.cols, (far, high, low, t)[k], N1, r2_x.at[k])
+            if k == 0:
+                cols = self.cols
+                self.c_up = send(self.one_of(far, N1, N2A), r2_low.at[:, :, cols], up)
+                self.c_down = send(self.one_of(far, N2A, 16), r2_high.at[:, :, cols], down)
+
+        def third_up(self):
             self.c_up.wait_recv()
-            add_one(cols, high, N1, r2_low)
-            self.e_up = send(self.one_of(high, N1, 16), r2_up.at[:, :, cols], up)
+            add_one(self.cols, high, N1, r2_low)
+            self.e_up = send(self.one_of(high, N1, 16), r2_up.at[:, :, self.cols], up)
+
+        def third_down(self):
             self.c_down.wait_recv()
-            add_one(cols, low, N2A, r2_high)
-            self.e_down = send(self.one_of(low, N1, 16), r2_down.at[:, :, cols], down)
+            add_one(self.cols, low, N2A, r2_high)
+            self.e_down = send(self.one_of(low, N1, 16), r2_down.at[:, :, self.cols], down)
 
         def fold(self):
             cols = self.cols
@@ -465,47 +473,46 @@
                 partial[at] = (total + r1_down[1 - xh, i, :, cols].astype(F32)).astype(BF16)
                 return carry
 
-            lax.fori_loop(0, N1, step, 0)
+            lax.fori_loop(0, N1, step, 0, unroll=3)
             self.ex = send(self.one_of(there, 0, N1), r1_x.at[:, :, cols], partner)
 
-        def finish(self, sx):
+        def finish_two(self):
             cols = self.cols
-            sx[3].wait_recv()
-            add_one(cols, t, N1, r2_x.at[3])
             self.e_up.wait_recv()
             self.e_down.wait_recv()
 
-            def two(i, carry):
+            def step(i, carry):
                 at = (t, N1 + i, slice(None), cols)
                 total = partial[at].astype(F32) + r2_up[i, :, cols].astype(F32)
                 partial[at] = (total + r2_down[i, :, cols].astype(F32)).astype(BF16)
                 return carry
 
-            lax.fori_loop(0, 16 - N1, two, 0)
+            lax.fori_loop(0, 16 - N1, step, 0, unroll=True)
+
+        def finish_one(self):
+            cols = self.cols
             self.ex.wait_recv()
 
-            def one(i, carry):
+            def step(i, carry):
                 at = (t, i, slice(None), cols)
                 total = partial[at].astype(F32) + r1_up[xh, i, :, cols].astype(F32)
                 total = total + r1_down[xh, i, :, cols].astype(F32)
                 partial[at] = (total + r1_x[i, :, cols].astype(F32)).astype(BF16)
                 return carry
 
-            lax.fori_loop(0, N1, one, 0)
+            lax.fori_loop(0, N1, step, 0, unroll=3)
 
         def relay(self):
             cols = self.cols
-            copies = []
             for k in range(16):
                 device = dp_peer(k)[1]
                 if k == 0:
                     landed[b, :, cols] = partial[t, chosen[k], :, cols]
                 else:
                     staged[k, :, cols] = partial[t, chosen[k], :, cols]
-                    copies.append(
+                    self.copies.append(
                         send(staged.at[k, :, cols], landed.at[b, :, cols], device)
                     )
-            return copies
 
         def score(self):
             cols = self.cols
@@ -528,26 +535,25 @@
             pair = jnp.where(destination[b * 16 + j] == index, j, pair)
         chosen.append(pair)
 
-    h0, h1 = Half(0), Half(1)
-    h0.begin()
-    sx0 = [h0.cross(k) for k in range(4)]
-    h1.begin()
-    sx1 = [h1.cross(0)]
-    h0.middle()
-    h0.second(sx0)
-    h0.third()
-    h0.fold()
-    sx1 += [h1.cross(k) for k in range(1, 4)]
-    h1.middle()
-    h0.finish(sx0)
-    pair_copies = h0.relay()
-    h0.score()
-    h1.second(sx1)
-    h1.third()
-    h1.fold()
-    h1.finish(sx1)
-    pair_copies += h1.relay()
-    h1.score()
+    halves = (Half(0), Half(1))
+    steps = {
+        "b": Half.begin,
+        "mu": Half.mid_up,
+        "md": Half.mid_down,
+        "tu": Half.third_up,
+        "td": Half.third_down,
+        "fo": Half.fold,
+        "f2": Half.finish_two,
+        "f1": Half.finish_one,
+        "re": Half.relay,
+        "sc": Half.score,
+    }
+    for k in range(4):
+        steps[f"x{k}"] = functools.partial(Half.cross, k=k)
+        steps[f"s{k}"] = functools.partial(Half.crossed, k=k)
+    for name, h in ORDER:
+        steps[name](halves[h])
+    pair_copies = halves[0].copies + halves[1].copies
 
     mean = (squares[0] + squares[1]) / D
     score_one[...] = (dots[0] + dots[1]) * lax.rsqrt(mean + norm_eps)

time: 164 us -> 149 us (0.909)
  Pallas kernels: 158 us -> 143 us
    pallas_call x1, Pallas kernels: 158 us -> 143 us  [on_device(): pl.pallas_call(layer_kernel, out_shape=[jax.ShapeDtypeStruct((16, 16, D),...]
where the time goes in v3:
time: 149 us
  Pallas kernels  143 us (96%)
  local copies, waits for them, and re-layouts  4.3 us (3%)
    pallas_call x1, Pallas kernels, on_device(): pl.pallas_call(layer_kernel, out_shape=[jax.ShapeDtypeStruct((16, 16, D),...  143 us

profile of v3, /device:TPU:1, one launch (start us, length us, event | category | flops | bytes accessed | tf_op | source)
XLA Modules:
  0.0 148.5 jit_solution(4745730229076313249)
XLA Ops:
  0.6 0.0 copy-start.1
  0.7 0.0 copy-start
  0.7 142.7 %shard_map.202 = (bf16[16,16,1536]{2,1,0:T(8,128)(2,1)}, f32[16,16,128]{2,1,0:T(8,128)}) custom-call(s32[256]{0:T(256)} %lengths.1, s32[256]{0:T(256)} %destination.1, f32[1536]{0:T(1024)} %gain.1, f32[1536]{0:T(1024)} %mlp_gain.1, f32[1536]{0:T(1024)} %final_gain.1, f32[1536]{0:T(1024)} %score_weight.1, bf16[128]{0:T(256)(128)(2,1)} %q_bias.1, ...), custom_call_target="tpu_custom_call" | custom-call | tf_op jit(solution)/shard_map/pallas_call | solution.py:608
  143.4 1.0 slice_reduce_fusion
  144.4 0.1 broadcast_in_dim.31
  144.5 0.0 copy-done.1
  144.5 0.1 select_reduce_fusion.1
  144.6 0.6 dynamic_slice.3
  145.2 0.0 copy-done
  145.2 0.1 reshape.17
  145.3 0.1 select_reduce_fusion
  145.4 0.1 reduce_sum.31
  145.5 0.6 select_reduce_fusion.2
  146.1 2.4 %copy.24 = bf16[16,16,1536]{2,1,0:T(8,128)(2,1)} copy(bf16[16,16,1536]{2,0,1:T(8,128)(2,1)} %bitcast.5) | data formatting | bytes 1572864
  (2 shorter events, 0.0 us)
Async XLA Ops:
  0.6 143.8 %copy-start.1 = (s32[256]{0:T(256)S(1)}, s32[256]{0:T(256)}, u32[]{:S(2)}) copy-start(s32[256]{0:T(256)} %param.21) | copy-start | bytes 3076
  0.7 144.5 %copy-start = (s32[256]{0:T(256)S(1)}, s32[256]{0:T(256)}, u32[]{:S(2)}) copy-start(s32[256]{0:T(256)} %destination.1) | copy-start | bytes 3076

commit v4 on v3

--- a/solution.py
+++ b/solution.py
@@ -44,8 +44,11 @@
     ("mu", 0), ("s0", 0), ("x1", 1), ("md", 1), ("x0", 1), ("mu", 1), ("fo", 0), ("s0", 1),
     ("s2", 1), ("s1", 0), ("s3", 0), ("tu", 0), ("s2", 0), ("td", 0), ("x3", 1), ("s1", 1),
     ("td", 1), ("fo", 1), ("tu", 1), ("s3", 1), ("f1", 0), ("f2", 0), ("re", 0), ("sc", 0),
-    ("f1", 1), ("f2", 1), ("re", 1), ("sc", 1),
+    ("f1", 1), ("f2", 1), ("sc", 1),
 )
+
+
+EARLY = 5
 
 
 def z_at(step):
@@ -89,13 +92,6 @@
     return index, {"y": index // 4, "xl": lax.rem(index // 2, 2), "c": lax.rem(index, 2)}
 
 
-def greet(devices):
-    barrier = pltpu.get_barrier_semaphore()
-    for device in devices:
-        pl.semaphore_signal(barrier, inc=1, device_id=device, device_id_type=MESH)
-    pl.semaphore_wait(barrier, len(devices))
-
-
 def rms_rows(values, gain):
     scale = lax.rsqrt(jnp.mean(values * values, axis=-1, keepdims=True) + norm_eps)
     return values * scale * gain
@@ -106,13 +102,15 @@
 
 
 def layer_kernel(
-    lengths, destination, gain, mlp_gain, final_gain, score_weight, q_bias, v_bias, cosine, sine,
+    lengths, destination, q_bias, v_bias,
+    gain_in, mlp_gain_in, final_gain_in, score_weight_in, cosine_in, sine_in,
     arrived, q_w, k_w, v_w, o_w, w_gate, w_up, w_down,
     relaid_out, scores_out,
+    gain, mlp_gain, final_gain, score_weight, cosine, sine,
     x_v, k_v, v_v, q_all, o_all, bias_one, bias_all, normed, keys, values, queries, context,
     after_v, gathered, wg, wu, wd, w_tail, active, partial,
     r1_low, r1_high, r1_up, r1_down, r1_x, r2_x, r2_low, r2_high, r2_up, r2_down,
-    staged, landed, squares, dots, score_one, score_eight, score_sum, score_all,
+    staged, landed, last_rows, squares, dots, score_one, score_eight, score_sum, score_all,
     local_sem, send_sem, recv_sem,
 ):
     z, xh, c = lax.axis_index("z"), lax.axis_index("xh"), lax.axis_index("c")
@@ -141,14 +139,24 @@
         (w_down, wd.at[pl.ds(0, FFL)]),
         (w_gate.at[pl.ds(FULL, TAIL)], w_tail.at[pl.ds(0, TAIL)]),
         (w_up.at[pl.ds(FULL, TAIL)], w_tail.at[pl.ds(128, TAIL)]),
+        (gain_in, gain),
+        (cosine_in, cosine),
+        (sine_in, sine),
+        (mlp_gain_in, mlp_gain),
+        (final_gain_in, final_gain),
+        (score_weight_in, score_weight),
     ]
     loads = [
         pltpu.make_async_copy(src, dst, local_sem.at[i]) for i, (src, dst) in enumerate(sources)
     ]
-    for load in loads[:5]:
-        load.start()
+    peers = [tensor_peer(k) for k in range(1, 8)] + [dp_peer(k)[1] for k in range(1, 16)]
+    barrier = pltpu.get_barrier_semaphore()
+    for device in peers:
+        pl.semaphore_signal(barrier, inc=1, device_id=device, device_id_type=MESH)
+    for i in (3, 4, 0, 1, 2, *range(10, 16)):
+        loads[i].start()
     bias_one[...] = jnp.broadcast_to(q_bias[...].reshape(1, HEAD_DIM).astype(F32), bias_one.shape)
-    greet([tensor_peer(k) for k in range(1, 8)] + [dp_peer(k)[1] for k in range(1, 16)])
+    pl.semaphore_wait(barrier, len(peers))
     send = Sender(send_sem, recv_sem)
 
     half_q, half_o = D // 2, HEAD_DIM // 2
@@ -163,18 +171,21 @@
         start = index * HEAD_DIM + c * half_o + (0 if sub is None else sub * size)
         return o_all.at[pl.ds(pl.multiple_of(start, 32), size)]
 
-    own_q = q_w.at[pl.ds(pl.multiple_of(c * half_q, 128), half_q)]
-    own_o = o_w.at[pl.ds(pl.multiple_of(c * half_o, 64), half_o)]
+    own_q, own_o = q_piece(t), o_piece(t)
+    loads[3].wait()
+    loads[4].wait()
 
     o_u, o_d = send(own_o, o_piece(t), up), send(own_o, o_piece(t), down)
     q_x = send(own_q, q_piece(t), partner)
     q_u, q_d = send(own_q, q_piece(t), up), send(own_q, q_piece(t), down)
     bias_copies = [send(bias_one, bias_all.at[t], tensor_peer(k)) for k in range(1, 8)]
     o_x = send(own_o, o_piece(t), partner)
-    for load in loads[5:]:
+    for load in loads[5:10]:
         load.start()
 
     loads[0].wait()
+    for load in loads[10:]:
+        load.wait()
     x = x_v[...].reshape(2 * SEQ, D)
     normed[...] = rms_rows(x.astype(F32), gain[...].reshape(1, D)).astype(BF16)
     loads[1].wait()
@@ -189,6 +200,14 @@
     values[...] = (v_f + v_bias[...].reshape(1, -1).astype(F32)).astype(BF16)
 
     q_sib, o_sib = [], []
+
+    def project_q(i):
+        cols = pl.ds(pl.multiple_of(i * 256, 256), 256)
+        q_f = jnp.dot(normed[...], q_all[:, cols], preferred_element_type=F32)
+        for e in range(2):
+            q_e = q_f[:, e * HEAD_DIM : (e + 1) * HEAD_DIM] + bias_all[2 * i + e][0:1]
+            at = pl.ds(pl.multiple_of(i * 256 + e * HEAD_DIM, HEAD_DIM), HEAD_DIM)
+            queries[:, at] = rotate(q_e, cos_rows, sin_rows).astype(BF16)
 
     def share(piece, index, sub, copies):
         copies.append(send(piece(index, sub), piece(index, sub), sibling))
@@ -222,6 +241,11 @@
     share(o_piece, far, 1, o_sib)
     o_x.wait_recv()
     share(o_piece, there, None, o_sib)
+    for copy in bias_copies:
+        copy.wait_recv()
+    bias_all[t] = bias_one[...]
+    q_sib[0].wait_recv()
+    project_q(z)
     q_xu.wait_recv()
     q_fxu = pass_piece(q_piece, low_x, 0, up)
     share(q_piece, low_x, None, q_sib)
@@ -236,27 +260,17 @@
     share(q_piece, far, 1, q_sib)
     o_xh.wait_recv()
     share(o_piece, high_x, None, o_sib)
+    for copy in q_sib[1:5]:
+        copy.wait_recv()
+    project_q(zm)
+    project_q(zp)
     q_fxu.wait_recv()
     share(q_piece, far_x, 0, q_sib)
     q_fxd.wait_recv()
     share(q_piece, far_x, 1, q_sib)
-    for copy in q_sib:
+    for copy in q_sib[5:]:
         copy.wait_recv()
-    loads[3].wait()
-    for copy in bias_copies:
-        copy.wait_recv()
-    bias_all[t] = bias_one[...]
-
-    def project_q(i, carry):
-        cols = pl.ds(pl.multiple_of(i * 256, 256), 256)
-        q_f = jnp.dot(normed[...], q_all[:, cols], preferred_element_type=F32)
-        for e in range(2):
-            q_e = q_f[:, e * HEAD_DIM : (e + 1) * HEAD_DIM] + bias_all[2 * i + e][0:1]
-            at = pl.ds(pl.multiple_of(i * 256 + e * HEAD_DIM, HEAD_DIM), HEAD_DIM)
-            queries[:, at] = rotate(q_e, cos_rows, sin_rows).astype(BF16)
-        return carry
-
-    lax.fori_loop(0, HEADS // 2, project_q, 0, unroll=True)
+    project_q(z2)
 
     o_xfa.wait_recv()
     share(o_piece, far_x, 0, o_sib)
@@ -267,7 +281,10 @@
     k_pos = lax.broadcasted_iota(jnp.int32, (SEQ, SEQ), 1)
     group = HEADS // KV_HEADS
     first_pair = (b * 8 + t) * 2
-    for p in range(2):
+    for copy in o_sib:
+        copy.wait_recv()
+
+    def attend(p):
         rows = slice(p * SEQ, (p + 1) * SEQ)
         allowed = (k_pos <= q_pos) & (k_pos < lengths[first_pair + p])
         allowed = jnp.concatenate([allowed.astype(F32)] * group, axis=0) > 0.5
@@ -290,20 +307,12 @@
             for h in range(group):
                 at = (g * group + h) * HEAD_DIM
                 context[rows, at : at + HEAD_DIM] = ctx[h * SEQ : (h + 1) * SEQ]
-
-    for copy in o_sib:
-        copy.wait_recv()
-    loads[4].wait()
-
-    def project_out(i, carry):
-        cols = pl.ds(pl.multiple_of(i * 256, 256), 256)
-        attended = jnp.dot(context[...], o_all[:, cols], preferred_element_type=F32)
-        base = x_v[:, :, cols].reshape(2 * SEQ, 256).astype(F32)
-        after_v[:, cols] = (base + attended).astype(BF16)
-        return carry
-
-    lax.fori_loop(0, D // 256, project_out, 0, unroll=True)
-    gathered[t] = rms_rows(after_v[...].astype(F32), mlp_gain[...].reshape(1, D)).astype(BF16)
+        for i in range(D // 256):
+            cols = slice(i * 256, (i + 1) * 256)
+            attended = jnp.dot(context[rows], o_all[:, cols], preferred_element_type=F32)
+            after_v[rows, cols] = (x_v[p, :, cols].astype(F32) + attended).astype(BF16)
+        after_rows = after_v[rows].astype(F32)
+        gathered[t, rows] = rms_rows(after_rows, mlp_gain[...].reshape(1, D)).astype(BF16)
 
     def block_rows(g, span):
         return gathered.at[g, pl.ds(span[0], span[1] - span[0])]
@@ -311,14 +320,16 @@
     def pass_on(g, span, device):
         return send(block_rows(g, span), block_rows(g, span), device)
 
+    attend(1)
     u2 = pass_on(here, C2, up)
     d2 = pass_on(here, C2, down)
-    x1 = pass_on(here, C1, partner)
+    x2 = pass_on(here, C2, partner)
+    attend(0)
     u1 = pass_on(here, C1, up)
     d1 = pass_on(here, C1, down)
-    x2 = pass_on(here, C2, partner)
-
-    for load in loads[5:]:
+    x1 = pass_on(here, C1, partner)
+
+    for load in loads[5:10]:
         load.wait()
     wd[FFL:FFP] = jnp.zeros((FFP - FFL, D), BF16)
     w_tail[TAIL:128] = jnp.zeros((128 - TAIL, D), BF16)
@@ -332,7 +343,7 @@
             gathered[g], weights, (((1,), (1,)), ((), ())), preferred_element_type=F32
         )
 
-    def block(g, own=False):
+    def block(g, own=False, between=None):
         def hidden(i, carry):
             at = pl.ds(pl.multiple_of(i * 256, 256), 256)
             active[:, at] = gated(by_rows(g, wg[at]), by_rows(g, wu[at]))
@@ -342,17 +353,16 @@
         both = by_rows(g, w_tail[...])
         active[:, FULL:FFP] = gated(both[:, :128], both[:, 128:])
 
-        def project(i, carry):
-            cols = pl.ds(pl.multiple_of(i * 256, 256), 256)
+        for i in range(D // 256):
+            if i == D // 512 and between is not None:
+                between()
+            cols = slice(i * 256, (i + 1) * 256)
             result = jnp.dot(active[...], wd[:, cols], preferred_element_type=F32)
             if own:
                 result = result.astype(BF16).astype(F32) + after_v[:, cols].astype(F32)
             result = result.astype(BF16).reshape(2, 8, 16, 256)
             for owner in range(8):
                 partial[owner, pl.ds(2 * g, 2), :, cols] = result[:, owner]
-            return carry
-
-        lax.fori_loop(0, D // 256, project, 0, unroll=True)
 
     block(here, own=True)
     u2.wait_recv()
@@ -391,7 +401,6 @@
     fxd.wait_recv()
     x_far_a.wait_recv()
     x_far_b.wait_recv()
-    block(far_x)
 
     def add_both(cols, zz, lo, extra):
         def step(i, carry):
@@ -521,11 +530,12 @@
             for p in range(16):
                 wanted = lengths[b * 16 + p] - 1 - t * 16
                 row = jnp.where(position == wanted, partial[t, p, :, cols].astype(F32), 0.0)
-                row = jnp.sum(row, axis=0, keepdims=True)
-                sums = jnp.sum(row * row, axis=-1, keepdims=True)
-                squares[self.h, p : p + 1] = jnp.broadcast_to(sums, (1, 128))
-                sums = jnp.sum(row * weight, axis=-1, keepdims=True)
-                dots[self.h, p : p + 1] = jnp.broadcast_to(sums, (1, 128))
+                last_rows[p : p + 1] = jnp.sum(row, axis=0, keepdims=True)
+            found = last_rows[...]
+            sums = jnp.sum(found * found, axis=-1, keepdims=True)
+            squares[self.h] = jnp.broadcast_to(sums, (16, 128))
+            sums = jnp.sum(found * weight, axis=-1, keepdims=True)
+            dots[self.h] = jnp.broadcast_to(sums, (16, 128))
 
     chosen = []
     for k in range(16):
@@ -551,14 +561,19 @@
     for k in range(4):
         steps[f"x{k}"] = functools.partial(Half.cross, k=k)
         steps[f"s{k}"] = functools.partial(Half.crossed, k=k)
-    for name, h in ORDER:
+    def begin_first():
+        for name, h in ORDER[:EARLY]:
+            steps[name](halves[h])
+
+    block(far_x, between=begin_first)
+    for name, h in ORDER[EARLY:]:
         steps[name](halves[h])
-    pair_copies = halves[0].copies + halves[1].copies
 
     mean = (squares[0] + squares[1]) / D
     score_one[...] = (dots[0] + dots[1]) * lax.rsqrt(mean + norm_eps)
     copies = [send(score_one, score_eight.at[t], tensor_peer(k)) for k in range(1, 8)]
     score_eight[t] = score_one[...]
+    halves[1].relay()
     for copy in copies:
         copy.wait_recv()
     total = score_eight[0]
@@ -567,13 +582,23 @@
     score_sum[...] = total
     score_all[b] = total
     copies = [send(score_sum, score_all.at[b], dp_peer(k)[1]) for k in range(1, 16)]
+    writes = []
+
+    def write(src, dst):
+        copy = pltpu.make_async_copy(src, dst, local_sem.at[len(loads) + len(writes)])
+        copy.start()
+        writes.append(copy)
+
+    for half in halves:
+        for copy in half.copies:
+            copy.wait_recv()
+        write(landed.at[:, :, half.cols], relaid_out.at[:, :, half.cols])
     for copy in copies:
         copy.wait_recv()
-    scores_out[...] = score_all[...]
-    for copy in pair_copies:
-        copy.wait_recv()
-    relaid_out[...] = landed[...]
+    write(score_all, scores_out)
     send.drain()
+    for copy in writes:
+        copy.wait()
 
 
 def any_spec():
@@ -611,9 +636,15 @@
             jax.ShapeDtypeStruct((16, 16, D), BF16),
             jax.ShapeDtypeStruct((16, 16, 128), F32),
         ],
-        in_specs=[smem_spec()] * 2 + [vmem_spec()] * 8 + [any_spec()] * 8,
-        out_specs=[vmem_spec()] * 2,
+        in_specs=[smem_spec()] * 2 + [vmem_spec()] * 2 + [any_spec()] * 14,
+        out_specs=[any_spec()] * 2,
         scratch_shapes=[
+            pltpu.VMEM((D,), F32),
+            pltpu.VMEM((D,), F32),
+            pltpu.VMEM((D,), F32),
+            pltpu.VMEM((D,), F32),
+            pltpu.VMEM((SEQ, HEAD_DIM), F32),
+            pltpu.VMEM((SEQ, HEAD_DIM), F32),
             pltpu.VMEM((2, SEQ, D), BF16),
             pltpu.VMEM((D, KV_HEADS * HEAD_DIM), BF16),
             pltpu.VMEM((D, KV_HEADS * HEAD_DIM), BF16),
@@ -646,13 +677,14 @@
             pairs(16 - N1),
             pairs(16),
             pairs(16),
+            pltpu.VMEM((16, D // 2), F32),
             pltpu.VMEM((2, 16, 128), F32),
             pltpu.VMEM((2, 16, 128), F32),
             pltpu.VMEM((16, 128), F32),
             pltpu.VMEM((8, 16, 128), F32),
             pltpu.VMEM((16, 128), F32),
             pltpu.VMEM((16, 16, 128), F32),
-            pltpu.SemaphoreType.DMA((10,)),
+            pltpu.SemaphoreType.DMA((19,)),
             pltpu.SemaphoreType.DMA((144,)),
             pltpu.SemaphoreType.DMA((144,)),
         ],
@@ -660,7 +692,7 @@
             collective_id=0, has_side_effects=True, vmem_limit_bytes=60 * 2**20
         ),
     )(
-        lengths, destination, attn_gain, mlp_gain, final_gain, score_weight, q_bias, v_bias,
+        lengths, destination, q_bias, v_bias, attn_gain, mlp_gain, final_gain, score_weight,
         cosine, sine, arrived, q_weight, k_weight, v_weight, o_weight, w_gate.T, w_up.T, w_down,
     )
     hidden_out = jnp.transpose(relaid, (1, 0, 2))

time: 149 us -> 144 us (0.966)
  Pallas kernels: 143 us -> 138 us
    pallas_call x1, Pallas kernels: 143 us -> 138 us  [on_device(): pl.pallas_call(layer_kernel, out_shape=[jax.ShapeDtypeStruct((16, 16, D),...]
where the time goes in v4:
time: 144 us
  Pallas kernels  138 us (96%)
  local copies, waits for them, and re-layouts  4.3 us (3%)
    pallas_call x1, Pallas kernels, on_device(): pl.pallas_call(layer_kernel, out_shape=[jax.ShapeDtypeStruct((16, 16, D),...  138 us

profile of v4, /device:TPU:1, one launch (start us, length us, event | category | flops | bytes accessed | tf_op | source)
XLA Modules:
  0.0 144.0 jit_solution(12295123593301277593)
XLA Ops:
  0.6 0.0 copy-start.1
  0.7 0.0 copy-start
  0.7 138.1 %shard_map.202 = (bf16[16,16,1536]{2,1,0:T(8,128)(2,1)}, f32[16,16,128]{2,1,0:T(8,128)}) custom-call(s32[256]{0:T(256)} %lengths.1, s32[256]{0:T(256)} %destination.1, bf16[128]{0:T(256)(128)(2,1)} %q_bias.1, bf16[256]{0:T(256)(128)(2,1)} %v_bias.1, f32[1536]{0:T(1024)} %gain_in.1, f32[1536]{0:T(1024)} %mlp_gain_in.1, f32[1536]{0:T(1024)} %final_gain_in.1, ...), custom_call_target="tpu_custom_call" | custom-call | tf_op jit(solution)/shard_map/pallas_call | solution.py:633
  138.8 1.0 slice_reduce_fusion
  139.8 0.1 broadcast_in_dim.31
  139.9 0.0 copy-done.1
  139.9 0.1 select_reduce_fusion.1
  140.0 0.6 dynamic_slice.3
  140.6 0.0 copy-done
  140.6 0.1 reshape.17
  140.7 0.1 select_reduce_fusion
  140.8 0.1 reduce_sum.31
  140.9 0.6 select_reduce_fusion.2
  141.5 2.4 %copy.24 = bf16[16,16,1536]{2,1,0:T(8,128)(2,1)} copy(bf16[16,16,1536]{2,0,1:T(8,128)(2,1)} %bitcast.5) | data formatting | bytes 1572864
  (2 shorter events, 0.0 us)
Async XLA Ops:
  0.6 139.3 %copy-start.1 = (s32[256]{0:T(256)S(1)}, s32[256]{0:T(256)}, u32[]{:S(2)}) copy-start(s32[256]{0:T(256)} %param.21) | copy-start | bytes 3076
  0.7 140.0 %copy-start = (s32[256]{0:T(256)S(1)}, s32[256]{0:T(256)}, u32[]{:S(2)}) copy-start(s32[256]{0:T(256)} %destination.1) | copy-start | bytes 3076

commit v5 on v4

--- a/solution.py
+++ b/solution.py
@@ -166,10 +166,19 @@
         start = c * half_q + (0 if sub is None else sub * size)
         return q_all.at[pl.ds(pl.multiple_of(start, 128), size), q_cols(index)]
 
+    parity = lax.rem(y, 2)
+
+    def o_rows(index, side, sub):
+        size = half_o // 2 if sub is None else half_o // 4
+        start = index * HEAD_DIM + c * half_o + side * (half_o // 2)
+        start = start + (0 if sub is None else sub * size)
+        return o_all.at[pl.ds(pl.multiple_of(start, 16), size)]
+
     def o_piece(index, sub=None):
-        size = half_o if sub is None else half_o // 2
-        start = index * HEAD_DIM + c * half_o + (0 if sub is None else sub * size)
-        return o_all.at[pl.ds(pl.multiple_of(start, 32), size)]
+        return o_rows(index, parity, sub)
+
+    def o_other(index, sub):
+        return o_rows(index, 1 - parity, sub)
 
     own_q, own_o = q_piece(t), o_piece(t)
     loads[3].wait()
@@ -215,14 +224,31 @@
     def pass_piece(piece, index, sub, device):
         return send(piece(index, sub), piece(index, sub), device)
 
+    y_ahead = {"y": lax.rem(y + 1, 4)}
+    y_back = {"y": lax.rem(y + 3, 4)}
+    over_y = []
+
+    def spread(index, sub=None):
+        share(o_piece, index, sub, o_sib)
+        for part, device in ((0, y_ahead), (1, y_back)):
+            if sub is None or sub == part:
+                piece = o_piece(index, part)
+                over_y.append((send(piece, piece, device), index, part))
+
+    def collect(count):
+        for _ in range(count):
+            copy, index, part = over_y.pop(0)
+            copy.wait_recv()
+            share(o_other, index, part, o_sib)
+
     o_u.wait_recv()
     o_fu = pass_piece(o_piece, low, 0, up)
     o_xl = pass_piece(o_piece, low, None, partner)
-    share(o_piece, low, None, o_sib)
+    spread(low)
     o_d.wait_recv()
     o_fd = pass_piece(o_piece, high, 1, down)
     o_xh = pass_piece(o_piece, high, None, partner)
-    share(o_piece, high, None, o_sib)
+    spread(high)
     q_x.wait_recv()
     q_xu = pass_piece(q_piece, there, None, up)
     q_xd = pass_piece(q_piece, there, None, down)
@@ -233,49 +259,53 @@
     q_d.wait_recv()
     q_fd = pass_piece(q_piece, high, 1, down)
     share(q_piece, high, None, q_sib)
+    collect(4)
+    o_x.wait_recv()
+    spread(there)
     o_fu.wait_recv()
     o_xfa = pass_piece(o_piece, far, 0, partner)
-    share(o_piece, far, 0, o_sib)
+    spread(far, 0)
     o_fd.wait_recv()
     o_xfb = pass_piece(o_piece, far, 1, partner)
-    share(o_piece, far, 1, o_sib)
-    o_x.wait_recv()
-    share(o_piece, there, None, o_sib)
+    spread(far, 1)
     for copy in bias_copies:
         copy.wait_recv()
     bias_all[t] = bias_one[...]
     q_sib[0].wait_recv()
     project_q(z)
+    o_xl.wait_recv()
+    spread(low_x)
+    collect(4)
     q_xu.wait_recv()
     q_fxu = pass_piece(q_piece, low_x, 0, up)
     share(q_piece, low_x, None, q_sib)
     q_xd.wait_recv()
     q_fxd = pass_piece(q_piece, high_x, 1, down)
     share(q_piece, high_x, None, q_sib)
-    o_xl.wait_recv()
-    share(o_piece, low_x, None, o_sib)
+    o_xh.wait_recv()
+    spread(high_x)
+    collect(2)
     q_fu.wait_recv()
     share(q_piece, far, 0, q_sib)
     q_fd.wait_recv()
     share(q_piece, far, 1, q_sib)
-    o_xh.wait_recv()
-    share(o_piece, high_x, None, o_sib)
     for copy in q_sib[1:5]:
         copy.wait_recv()
     project_q(zm)
     project_q(zp)
+    o_xfa.wait_recv()
+    spread(far_x, 0)
+    o_xfb.wait_recv()
+    spread(far_x, 1)
+    collect(2)
     q_fxu.wait_recv()
     share(q_piece, far_x, 0, q_sib)
     q_fxd.wait_recv()
     share(q_piece, far_x, 1, q_sib)
+    collect(2)
     for copy in q_sib[5:]:
         copy.wait_recv()
     project_q(z2)
-
-    o_xfa.wait_recv()
-    share(o_piece, far_x, 0, o_sib)
-    o_xfb.wait_recv()
-    share(o_piece, far_x, 1, o_sib)
 
     q_pos = lax.broadcasted_iota(jnp.int32, (SEQ, SEQ), 0)
     k_pos = lax.broadcasted_iota(jnp.int32, (SEQ, SEQ), 1)
@@ -685,8 +715,8 @@
             pltpu.VMEM((16, 128), F32),
             pltpu.VMEM((16, 16, 128), F32),
             pltpu.SemaphoreType.DMA((19,)),
-            pltpu.SemaphoreType.DMA((144,)),
-            pltpu.SemaphoreType.DMA((144,)),
+            pltpu.SemaphoreType.DMA((176,)),
+            pltpu.SemaphoreType.DMA((176,)),
         ],
         compiler_params=pltpu.CompilerParams(
             collective_id=0, has_side_effects=True, vmem_limit_bytes=60 * 2**20

time: 144 us -> 142 us (0.986)
  Pallas kernels: 138 us -> 136 us
    pallas_call x1, Pallas kernels: 138 us -> 136 us  [on_device(): pl.pallas_call(layer_kernel, out_shape=[jax.ShapeDtypeStruct((16, 16, D),...]
where the time goes in v5:
time: 142 us
  Pallas kernels  136 us (96%)
  local copies, waits for them, and re-layouts  4.3 us (3%)
    pallas_call x1, Pallas kernels, on_device(): pl.pallas_call(layer_kernel, out_shape=[jax.ShapeDtypeStruct((16, 16, D),...  136 us

profile of v5, /device:TPU:1, one launch (start us, length us, event | category | flops | bytes accessed | tf_op | source)
XLA Modules:
  0.0 141.9 jit_solution(4441591012827579286)
XLA Ops:
  0.6 0.0 copy-start.1
  0.7 0.0 copy-start
  0.7 136.0 %shard_map.202 = (bf16[16,16,1536]{2,1,0:T(8,128)(2,1)}, f32[16,16,128]{2,1,0:T(8,128)}) custom-call(s32[256]{0:T(256)} %lengths.1, s32[256]{0:T(256)} %destination.1, bf16[128]{0:T(256)(128)(2,1)} %q_bias.1, bf16[256]{0:T(256)(128)(2,1)} %v_bias.1, f32[1536]{0:T(1024)} %gain_in.1, f32[1536]{0:T(1024)} %mlp_gain_in.1, f32[1536]{0:T(1024)} %final_gain_in.1, ...), custom_call_target="tpu_custom_call" | custom-call | tf_op jit(solution)/shard_map/pallas_call | solution.py:663
  136.7 1.0 slice_reduce_fusion
  137.7 0.1 broadcast_in_dim.31
  137.8 0.0 copy-done.1
  137.8 0.1 select_reduce_fusion.1
  137.9 0.6 dynamic_slice.3
  138.5 0.0 copy-done
  138.5 0.1 reshape.17
  138.6 0.1 select_reduce_fusion
  138.7 0.1 reduce_sum.31
  138.8 0.6 select_reduce_fusion.2
  139.4 2.4 %copy.24 = bf16[16,16,1536]{2,1,0:T(8,128)(2,1)} copy(bf16[16,16,1536]{2,0,1:T(8,128)(2,1)} %bitcast.5) | data formatting | bytes 1572864
  (2 shorter events, 0.0 us)
Async XLA Ops:
  0.6 137.2 %copy-start.1 = (s32[256]{0:T(256)S(1)}, s32[256]{0:T(256)}, u32[]{:S(2)}) copy-start(s32[256]{0:T(256)} %param.21) | copy-start | bytes 3076
  0.7 137.9 %copy-start = (s32[256]{0:T(256)S(1)}, s32[256]{0:T(256)}, u32[]{:S(2)}) copy-start(s32[256]{0:T(256)} %destination.1) | copy-start | bytes 3076

commit v6 on v5

--- a/solution.py
+++ b/solution.py
@@ -21,6 +21,7 @@
 HEAD_DIM = 128
 HEADS = 8
 QUERY_DP = 2
+PER_QUERY = 8
 theta_base = 1000000.0
 norm_eps = 1e-06
 
@@ -102,15 +103,16 @@
 
 
 def layer_kernel(
-    lengths, destination, q_bias, v_bias,
+    lengths, destination, query_of, q_bias, v_bias,
     gain_in, mlp_gain_in, final_gain_in, score_weight_in, cosine_in, sine_in,
     arrived, q_w, k_w, v_w, o_w, w_gate, w_up, w_down,
-    relaid_out, scores_out,
+    relaid_out, centred_out, mean_out,
     gain, mlp_gain, final_gain, score_weight, cosine, sine,
     x_v, k_v, v_v, q_all, o_all, bias_one, bias_all, normed, keys, values, queries, context,
     after_v, gathered, wg, wu, wd, w_tail, active, partial,
     r1_low, r1_high, r1_up, r1_down, r1_x, r2_x, r2_low, r2_high, r2_up, r2_down,
     staged, landed, last_rows, squares, dots, score_one, score_eight, score_sum, score_all,
+    query_rows, target_rows,
     local_sem, send_sem, recv_sem,
 ):
     z, xh, c = lax.axis_index("z"), lax.axis_index("xh"), lax.axis_index("c")
@@ -395,6 +397,13 @@
                 partial[owner, pl.ds(2 * g, 2), :, cols] = result[:, owner]
 
     block(here, own=True)
+
+    def tabulate(i, carry):
+        query_rows[pl.ds(i, 1)] = jnp.full((1, 128), query_of[i], jnp.int32)
+        target_rows[pl.ds(i, 1)] = jnp.full((1, 128), destination[i], jnp.int32)
+        return carry
+
+    lax.fori_loop(0, 256, tabulate, 0, unroll=8)
     u2.wait_recv()
     f2u = pass_on(low, C2A, up)
     x_low = pass_on(low, C2, partner)
@@ -619,13 +628,34 @@
         copy.start()
         writes.append(copy)
 
-    for half in halves:
+    def write_half(half):
         for copy in half.copies:
             copy.wait_recv()
         write(landed.at[:, :, half.cols], relaid_out.at[:, :, half.cols])
+
+    write_half(halves[0])
     for copy in copies:
         copy.wait_recv()
-    write(score_all, scores_out)
+    pair_scores = score_all[...].reshape(256, 128)
+    lane = lax.broadcasted_iota(jnp.int32, (256, 128), 1)
+    member = query_rows[...] == lane
+    means = jnp.sum(jnp.where(member, pair_scores, 0.0), axis=0, keepdims=True) / PER_QUERY
+    own_means = jnp.sum(jnp.where(member, means, 0.0), axis=1, keepdims=True)
+    mine = jnp.where(target_rows[...] == b, pair_scores - own_means, 0.0)
+    mine = jnp.sum(mine.reshape(16, 16, 128), axis=1)
+    at_row = lax.broadcasted_iota(jnp.int32, (16, 128), 0)
+    at_lane = lax.broadcasted_iota(jnp.int32, (16, 128), 1)
+    centred = jnp.sum(jnp.where(at_row == at_lane, mine, 0.0), axis=0, keepdims=True)
+    centred_out[...] = centred.reshape(128)[:16]
+    lane = lax.broadcasted_iota(jnp.int32, (1, 128), 1)
+    own = jnp.zeros((1, 128), F32)
+    for k in range(QUERY_DP):
+        mean = jnp.sum(
+            jnp.where(lane == b * QUERY_DP + k, means, 0.0), axis=1, keepdims=True
+        )
+        own = jnp.where(lane == k, mean, own)
+    mean_out[...] = own.reshape(128)[:QUERY_DP]
+    write_half(halves[1])
     send.drain()
     for copy in writes:
         copy.wait()
@@ -660,14 +690,15 @@
 ):
     cosine, sine = rotary_tables()
     pairs = lambda *lead: pltpu.VMEM((*lead, 16, D), BF16)
-    relaid, scores = pl.pallas_call(
+    relaid, centred, query_mean = pl.pallas_call(
         layer_kernel,
         out_shape=[
             jax.ShapeDtypeStruct((16, 16, D), BF16),
-            jax.ShapeDtypeStruct((16, 16, 128), F32),
+            jax.ShapeDtypeStruct((16,), F32),
+            jax.ShapeDtypeStruct((QUERY_DP,), F32),
         ],
-        in_specs=[smem_spec()] * 2 + [vmem_spec()] * 2 + [any_spec()] * 14,
-        out_specs=[any_spec()] * 2,
+        in_specs=[smem_spec()] * 3 + [vmem_spec()] * 2 + [any_spec()] * 14,
+        out_specs=[any_spec()] + [vmem_spec()] * 2,
         scratch_shapes=[
             pltpu.VMEM((D,), F32),
             pltpu.VMEM((D,), F32),
@@ -714,6 +745,8 @@
             pltpu.VMEM((8, 16, 128), F32),
             pltpu.VMEM((16, 128), F32),
             pltpu.VMEM((16, 16, 128), F32),
+            pltpu.VMEM((256, 128), jnp.int32),
+            pltpu.VMEM((256, 128), jnp.int32),
             pltpu.SemaphoreType.DMA((19,)),
             pltpu.SemaphoreType.DMA((176,)),
             pltpu.SemaphoreType.DMA((176,)),
@@ -722,22 +755,11 @@
             collective_id=0, has_side_effects=True, vmem_limit_bytes=60 * 2**20
         ),
     )(
-        lengths, destination, q_bias, v_bias, attn_gain, mlp_gain, final_gain, score_weight,
+        lengths, destination, query_of, q_bias, v_bias, attn_gain, mlp_gain, final_gain, score_weight,
         cosine, sine, arrived, q_weight, k_weight, v_weight, o_weight, w_gate.T, w_up.T, w_down,
     )
     hidden_out = jnp.transpose(relaid, (1, 0, 2))
 
-    group_index = lax.axis_index(DP)
-    pair_score = scores[:, :, 0].reshape(-1)
-    query_total = lax.axis_size(DP) * QUERY_DP
-    membership = query_of[:, None] == jnp.arange(query_total, dtype=jnp.int32)[None, :]
-    means = jnp.sum(jnp.where(membership, pair_score[:, None], 0.0), axis=0) / (
-        pair_score.shape[0] // query_total
-    )
-    own_mean = jnp.sum(jnp.where(membership, means[None, :], 0.0), axis=1)
-    here = (destination == group_index).reshape(16, 16)
-    centred = jnp.sum(jnp.where(here, (pair_score - own_mean).reshape(16, 16), 0.0), axis=1)
-    query_mean = lax.dynamic_slice_in_dim(means, group_index * QUERY_DP, QUERY_DP)
     return (hidden_out, centred, query_mean)
 
 

time: 142 us -> 142 us (level)
    unnamed x5 -> x3, local copies, waits for them, and re-layouts: 2.45 us -> 4.66 us
where the time goes in v6:
time: 142 us
  Pallas kernels  137 us (96%)
  local copies, waits for them, and re-layouts  4.66 us (3%)
    pallas_call x1, Pallas kernels, on_device(): pl.pallas_call(layer_kernel, out_shape=[jax.ShapeDtypeStruct((16, 16, D),...  137 us
    unnamed x3, local copies, waits for them, and re-layouts  4.66 us

profile of v6, /device:TPU:1, one launch (start us, length us, event | category | flops | bytes accessed | tf_op | source)
XLA Modules:
  0.0 142.0 jit_solution(7241522663880944522)
XLA Ops:
  0.6 136.7 %shard_map.202 = (bf16[16,16,1536]{2,1,0:T(8,128)(2,1)}, f32[16]{0:T(128)}, f32[2]{0:T(128)}) custom-call(s32[256]{0:T(256)} %lengths.1, s32[256]{0:T(256)} %destination.1, s32[256]{0:T(256)} %query_of.1, bf16[128]{0:T(256)(128)(2,1)} %q_bias.1, bf16[256]{0:T(256)(128)(2,1)} %v_bias.1, f32[1536]{0:T(1024)} %gain_in.1, f32[1536]{0:T(1024)} %mlp_gain_in.1, ...), custom_call_target="tpu_custom_call" | custom-call | tf_op jit(solution)/shard_map/pallas_call | solution.py:693
  137.3 2.4 %copy.22 = bf16[16,16,1536]{2,1,0:T(8,128)(2,1)} copy(bf16[16,16,1536]{2,0,1:T(8,128)(2,1)} %bitcast.5) | data formatting | bytes 1572864
  139.8 1.1 copy.25
  140.9 1.1 copy.26
